TPU v7x, 512 devices: a whole 4x8x8 slice. The times are simulated.
512 devices in a mesh: unit: 2 (over y_1), row: 16 (over y_0, x, core), col: 16 (over z, y_2).
Axes of the slice: x: 4, y: 8 (y_0: 2, y_1: 2, y_2: 2; y = y_0 * 4 + y_1 * 2 + y_2), z: 8, core: 2. Of those that a mesh axis runs over, the one named last changes fastest.
Arguments:
- tracer: float32 [4, 128, 256, 256], P('unit', None, 'row', 'col'), parts along dimension 0, may hold values from -6 to 6
- symbol_x: float32 [128], replicated, may hold values from 0.3 to 3
- symbol_y: float32 [256], replicated, may hold values from 0.3 to 3
- symbol_z: float32 [256], replicated, may hold values from 0.3 to 3
Outputs:
- smoothed: float32 [4, 128, 256, 256], P('unit', None, 'row', 'col'), parts along dimension 0
There are 2 independent parts, one for each index of `unit`. A program takes and returns all parts, laid end to end along the dimension named above; an argument that names none is the same for every part. Nothing has to cross between parts.
All inputs are finite; a program needn't handle non-finite values.
Results may differ from a plain program's by a relative error of at most 0.0003.
Values sent between devices are 32-bit elements.
A program may use at most 64 MiB of HBM per device.

v0:
```python
import functools

import jax
import jax.numpy as jnp
import numpy as np
from jax import lax
from jax.experimental import pallas as pl
from jax.experimental.pallas import tpu as pltpu
from jax.sharding import PartitionSpec as P

MESH = pl.DeviceIdType.MESH
LANES = 128
ROWS = 8


def mode_table(count):
    rank = np.arange(count)
    angle = np.pi / (4 * count) * ((2 * rank[:, None] + 1) * (2 * rank[None, :] + 1) % (8 * count))
    return np.cos(angle) * (2.0 / count) ** 0.5


def two_parts(table):
    high = table.astype(jnp.bfloat16)
    low = (table - high.astype(np.float64)).astype(jnp.bfloat16)
    return np.stack([high, low])


def split(values):
    high = values.astype(jnp.bfloat16)
    return high, (values - high.astype(jnp.float32)).astype(jnp.bfloat16)


def dot(a, b):
    return jnp.dot(a, b, preferred_element_type=jnp.float32)


def right(values, table):
    rows = values.shape[0]
    high, low = split(values)
    both = dot(jnp.concatenate([high, low], axis=0), table[0])
    return both[:rows] + (both[rows:] + dot(high, table[1]))


def left(table, values):
    high, low = split(values)
    return dot(table, jnp.concatenate([high, high, low], axis=0))


def swap_blocks(tiles):
    count = len(tiles)
    block = LANES // count
    which = lax.broadcasted_iota(jnp.int32, tiles[0].shape, 1) // block
    out = []
    for j in range(count):
        tile = tiles[j]
        for i in range(count):
            if i != j:
                moved = pltpu.roll(tiles[i], ((i - j) * block) % LANES, 1)
                tile = jnp.where(which == i, moved, tile)
        out.append(tile)
    return out


def middle(cols_n):
    if cols_n % 4:
        return 0, cols_n
    return cols_n // 4, cols_n // 2


def kernel(
    sizes, x_hbm, sx_ref, sy_hbm, sz_hbm, wx_hbm, wy_hbm, hz_hbm, recv_back,
    x_ref, sy_ref, sz_ref, wx_ref, wy_ref, hz_ref, send, recv, send_back,
    load_sem, send_sem, recv_sem, send_back_sem, recv_back_sem,
):
    fields, count_x, rows_n, cols_n, share_y, share_z, planes = sizes
    devices = rows_n * cols_n
    me = lax.axis_index("row") * cols_n + lax.axis_index("col")
    high_y, high_z = share_y // ROWS, share_z // ROWS
    groups = count_x // planes

    first_mid, mids = middle(cols_n)
    workers = rows_n * mids
    share = devices // workers
    row, col = lax.axis_index("row"), lax.axis_index("col")
    works = (col >= first_mid) & (col < first_mid + mids)
    idle = jnp.logical_not(works)
    mine = row * mids + jnp.clip(col - first_mid, 0, mids - 1)

    def place(index):
        return {"row": index // cols_n, "col": index % cols_n}

    def worker_place(index):
        return {"row": index // mids, "col": first_mid + index % mids}

    def each_worker(act):
        @pl.when(idle)
        def _():
            act(mine)

        for step in range(1, workers):
            act(lax.rem(mine + step, workers))

    def each_device(act):
        for step in range(1, devices):
            act(lax.rem(me + step, devices))

    barrier = pltpu.get_barrier_semaphore()

    def greet(where):
        pl.semaphore_signal(barrier, inc=1, device_id=where, device_id_type=MESH)

    each_worker(lambda index: greet(worker_place(index)))

    @pl.when(works)
    def _():
        for r in range(rows_n):
            for c in range(cols_n):
                if not first_mid <= c < first_mid + mids:
                    greet({"row": r, "col": c})

    loads = [
        pltpu.make_async_copy(source, target, load_sem.at[i])
        for i, (source, target) in enumerate(
            [
                (x_hbm, x_ref),
                (wx_hbm, wx_ref),
                (sy_hbm, sy_ref),
                (sz_hbm, sz_ref),
                (wy_hbm, wy_ref),
                (hz_hbm, hz_ref),
            ]
        )
    ]
    for load in loads[:2]:
        load.start()

    @pl.when(works)
    def _():
        for load in loads[2:]:
            load.start()

    def tiles_of(index):
        return pl.ds(index * share, share)

    def outward(worker, slot):
        return pltpu.make_async_remote_copy(
            src_ref=send.at[tiles_of(worker)],
            dst_ref=recv.at[tiles_of(slot)],
            send_sem=send_sem.at[worker],
            recv_sem=recv_sem.at[slot],
            device_id=worker_place(worker),
            device_id_type=MESH,
        )

    def homeward(peer, slot):
        return pltpu.make_async_remote_copy(
            src_ref=send_back.at[tiles_of(peer)],
            dst_ref=recv_back.at[tiles_of(slot)],
            send_sem=send_back_sem.at[peer],
            recv_sem=recv_back_sem.at[slot],
            device_id=place(peer),
            device_id_type=MESH,
        )

    loads[0].wait()
    loads[1].wait()
    packed = jnp.concatenate(
        [
            jnp.concatenate([x_ref[f * share_y + h * ROWS + y] for y in range(ROWS)], axis=1)
            for f in range(fields)
            for h in range(high_y)
        ],
        axis=0,
    )
    modes = right(packed, wx_ref)
    lane_tiles = count_x * ROWS // LANES
    per_tile = groups // lane_tiles

    def at(f, h, z, t):
        row = ((f * high_y + h) * high_z + z) * ROWS
        return modes[row : row + ROWS, t * LANES : (t + 1) * LANES]

    for f in range(fields):
        for t in range(lane_tiles):
            tiles = [at(f, h, z, t) for z in range(high_z) for h in range(high_y)]
            for i, tile in enumerate(swap_blocks(tiles)):
                send[f * groups + t * per_tile + i] = tile

    @pl.when(works)
    def _():
        pl.semaphore_wait(barrier, devices - 1)

    @pl.when(idle)
    def _():
        pl.semaphore_wait(barrier, workers)

    each_worker(lambda worker: outward(worker, me).start())

    @pl.when(works)
    def _():
        recv[tiles_of(me)] = send[tiles_of(mine)]
        for load in loads[2:]:
            load.wait()
        count_z, count_y = sz_ref.shape[1], sy_ref.shape[1]
        width = rows_n * high_y * planes * ROWS

        def column(row, size):
            diagonal = lax.broadcasted_iota(jnp.int32, (size, size), 0) == lax.broadcasted_iota(
                jnp.int32, (size, size), 1
            )
            return jnp.sum(jnp.where(diagonal, row, 0.0), axis=1, keepdims=True)

        symbol_z = column(sz_ref[...], count_z)
        lane = lax.broadcasted_iota(jnp.int32, (count_y, width), 1)
        rank = lane // (planes * ROWS) * ROWS + lane % ROWS
        chosen = rank == lax.broadcasted_iota(jnp.int32, (count_y, width), 0)
        symbol = jnp.sum(
            jnp.where(chosen, column(sy_ref[...], count_y), 0.0), axis=0, keepdims=True
        )
        plane = lax.broadcasted_iota(jnp.int32, (1, width), 1) // ROWS % planes
        factors = []
        for j in range(share):
            first = lax.rem(mine * share + j, groups) * planes
            symbol_x = jnp.zeros((1, width), jnp.float32)
            for p in range(planes):
                symbol_x = jnp.where(plane == p, sx_ref[first + p], symbol_x)
            factors.append(lax.rsqrt(symbol_x + symbol + symbol_z))
        factor = jnp.concatenate(factors, axis=1)

        each_device(lambda peer: outward(mine, peer).wait_recv())

        lane_tiles = width // LANES
        height = cols_n * high_z
        grid = [[None] * lane_tiles for _ in range(share * height)]
        for j in range(share):
            for c in range(cols_n):
                for t in range(lane_tiles):
                    tiles = [
                        recv[((t * high_z + i) * cols_n + c) * share + j] for i in range(high_z)
                    ]
                    for z, tile in enumerate(swap_blocks(tiles)):
                        grid[j * height + c * high_z + z][t] = tile
        block = jnp.concatenate([jnp.concatenate(row, axis=1) for row in grid], axis=0)
        block = right(block, wy_ref)
        block = jnp.concatenate(
            [block[j * count_z : (j + 1) * count_z] for j in range(share)], axis=1
        )
        block = left(hz_ref[...], block)
        block = block * factor
        block = left(hz_ref[...], block)
        block = jnp.concatenate(
            [block[:, j * width : (j + 1) * width] for j in range(share)], axis=0
        )
        block = right(block, wy_ref)
        for c in range(cols_n):
            for t in range(lane_tiles):
                for j in range(share):
                    start = [(j * height + c * high_z + z) * ROWS for z in range(high_z)]
                    tiles = [
                        block[at : at + ROWS, t * LANES : (t + 1) * LANES] for at in start
                    ]
                    for i, tile in enumerate(swap_blocks(tiles)):
                        send_back[((t * high_z + i) * cols_n + c) * share + j] = tile

        each_device(lambda peer: homeward(peer, mine).start())
        recv_back[tiles_of(mine)] = send_back[tiles_of(me)]

    each_worker(lambda worker: outward(worker, me).wait_send())
    each_worker(lambda worker: homeward(me, worker).wait_recv())

    @pl.when(works)
    def _():
        each_device(lambda peer: homeward(peer, mine).wait_send())


def finish(sizes, tiles_ref, wxt_ref, out_ref):
    fields, count_x, rows_n, cols_n, share_y, share_z, planes = sizes
    high_y, high_z = share_y // ROWS, share_z // ROWS
    groups = count_x // planes
    lane_tiles = count_x * ROWS // LANES
    per_tile = groups // lane_tiles
    grid = [[None] * lane_tiles for _ in range(fields * high_y * high_z)]
    for f in range(fields):
        for t in range(lane_tiles):
            tiles = [tiles_ref[f * groups + t * per_tile + i] for i in range(per_tile)]
            for i, tile in enumerate(swap_blocks(tiles)):
                z, h = divmod(i, high_y)
                grid[(f * high_y + h) * high_z + z][t] = tile
    modes = jnp.concatenate([jnp.concatenate(row, axis=1) for row in grid], axis=0)
    values = right(modes, wxt_ref)
    for f in range(fields):
        for h in range(high_y):
            row = (f * high_y + h) * share_z
            for y in range(ROWS):
                out_ref[f * share_y + h * ROWS + y] = values[
                    row : row + share_z, y * count_x : (y + 1) * count_x
                ]


def fused(sizes, tracer, symbol_x, symbol_y, symbol_z):
    fields, count_x, rows_n, cols_n, share_y, share_z, planes = sizes
    devices = rows_n * cols_n
    count_y, count_z = symbol_y.shape[0], symbol_z.shape[0]
    high_y = share_y // ROWS

    table_x = np.einsum("xk,ab->axkb", mode_table(count_x), np.eye(ROWS))
    table_x = table_x.reshape(ROWS * count_x, count_x * ROWS)
    blocks = rows_n * high_y
    table_y = np.einsum(
        "aybz,kl->akyblz",
        mode_table(count_y).reshape(blocks, ROWS, blocks, ROWS),
        np.eye(planes),
    ).reshape(blocks * planes * ROWS, blocks * planes * ROWS)
    high, low = two_parts(mode_table(count_z))
    table_z = np.concatenate([high, low, high], axis=1)

    values = jnp.transpose(tracer, (0, 2, 3, 1)).reshape(fields * share_y, share_z, count_x)
    hbm = pl.BlockSpec(memory_space=pltpu.HBM)
    vmem = pl.BlockSpec(memory_space=pltpu.VMEM)
    smem = pl.BlockSpec(memory_space=pltpu.SMEM)
    share = cols_n // middle(cols_n)[1]
    tiles = jax.ShapeDtypeStruct((devices, ROWS, LANES), jnp.float32)
    operands = (
        values,
        symbol_x,
        symbol_y.reshape(1, -1),
        symbol_z.reshape(1, -1),
        jnp.asarray(two_parts(table_x)),
        jnp.asarray(two_parts(table_y)),
        jnp.asarray(table_z),
    )
    held = [pltpu.VMEM(o.shape, o.dtype) for i, o in enumerate(operands) if i != 1]
    back = pl.pallas_call(
        functools.partial(kernel, sizes),
        out_shape=tiles,
        in_specs=[hbm, smem] + [hbm] * 5,
        out_specs=vmem,
        scratch_shapes=held
        + [pltpu.VMEM(tiles.shape, tiles.dtype)]
        + [pltpu.VMEM((devices * share, ROWS, LANES), jnp.float32)] * 2
        + [pltpu.SemaphoreType.DMA((len(held),))]
        + [pltpu.SemaphoreType.DMA((devices,))] * 4,
        compiler_params=pltpu.CompilerParams(
            collective_id=0, has_side_effects=True
        ),
    )(*operands)
    out = pl.pallas_call(
        functools.partial(finish, sizes),
        out_shape=jax.ShapeDtypeStruct(values.shape, jnp.float32),
        in_specs=[vmem, vmem],
        out_specs=vmem,
        compiler_params=pltpu.CompilerParams(),
    )(back, jnp.asarray(two_parts(table_x.T)))
    out = out.reshape(fields, share_y, share_z, count_x)
    return jnp.transpose(out, (0, 3, 1, 2))


def to_modes(values, dim):
    table = jnp.asarray(mode_table(values.shape[dim]), jnp.float32)
    moved = jnp.tensordot(values, table, axes=([dim], [0]), precision=lax.Precision.HIGHEST)
    return jnp.moveaxis(moved, -1, dim)


def by_lines(values, symbol_x, symbol_y, symbol_z):
    values = to_modes(values, 1)
    values = lax.all_to_all(values, "row", split_axis=1, concat_axis=2, tiled=True)
    values = to_modes(values, 2)
    values = lax.all_to_all(values, "col", split_axis=2, concat_axis=3, tiled=True)
    values = to_modes(values, 3)
    share_x, share_y = values.shape[1], values.shape[2]
    part_x = lax.dynamic_slice_in_dim(symbol_x, lax.axis_index("row") * share_x, share_x)
    part_y = lax.dynamic_slice_in_dim(symbol_y, lax.axis_index("col") * share_y, share_y)
    symbol = part_x[:, None, None] + part_y[None, :, None] + symbol_z[None, None, :]
    values = values * lax.rsqrt(symbol)
    values = to_modes(values, 3)
    values = lax.all_to_all(values, "col", split_axis=3, concat_axis=2, tiled=True)
    values = to_modes(values, 2)
    values = lax.all_to_all(values, "row", split_axis=2, concat_axis=1, tiled=True)
    return to_modes(values, 1)


def solution(mesh):
    rows_n, cols_n = mesh.shape["row"], mesh.shape["col"]

    def shards(tracer, symbol_x, symbol_y, symbol_z):
        fields, count_x, share_y, share_z = tracer.shape
        planes = fields * count_x // (rows_n * cols_n)
        high_y, high_z = share_y // ROWS, share_z // ROWS
        whole_tiles = (
            planes * rows_n * cols_n == fields * count_x
            and planes > 0
            and count_x % planes == 0
            and high_y * ROWS == share_y
            and high_z * ROWS == share_z
            and planes * ROWS * high_y * high_z == LANES
            and count_x * ROWS % LANES == 0
            and rows_n % high_z == 0
            and count_x // planes % (cols_n // middle(cols_n)[1]) == 0
        )
        if not whole_tiles:
            return by_lines(tracer, symbol_x, symbol_y, symbol_z)
        sizes = fields, count_x, rows_n, cols_n, share_y, share_z, planes
        return fused(sizes, tracer, symbol_x, symbol_y, symbol_z)

    in_specs = (P("unit", None, "row", "col"), P(), P(), P())
    out_specs = P("unit", None, "row", "col")
    return jax.shard_map(shards, mesh=mesh, in_specs=in_specs, out_specs=out_specs, check_vma=False)
```

profile of v0, /device:TPU:8, one launch (start us, length us, event | category | flops | bytes accessed | tf_op | source)
XLA Modules:
  0.0 121.6 jit_solution(5998472489402224273)
XLA Ops:
  0.0 0.9 copy-done
  1.0 1.2 fusion
  2.2 1.8 %copy.19 = f32[2,128,16,16]{3,2,0,1:T(8,128)S(1)} copy(f32[2,128,16,16]{1,3,2,0:T(8,128)S(1)} %bitcast.70) | data formatting | bytes 524288 | tf_op jit(solution)/shard_map/transpose | solution.py:361
  4.0 0.8 reshape.48
  4.8 23.7 %all_to_all.72 = f32[16,1,4096]{2,1,0:T(1,128)S(1)} all-to-all(f32[16,1,4096]{2,1,0:T(1,128)S(1)} %reshape.48), channel_id=1, replica_groups=mesh['unit'=2,'row'=16,'col'=16] {'row'}, dimensions={0} | all-to-all | bytes 524288 | tf_op jit(solution)/shard_map/all_to_all | solution.py:366
  29.0 1.2 %reduce = f32[16,4096]{1,0:T(8,128)S(1)} reduce(f32[16,1,4096]{2,1,0:T(1,128)S(1)} %all_to_all.72, f32[]{:T(128)} %broadcast.32), dimensions={1}, to_apply=%all_to_all.52.reduce_sub_computation | reduce | bytes 524292 | tf_op jit(solution)/shard_map/all_to_all | solution.py:366
  30.2 0.7 reshape.49
  31.0 2.0 %copy.21 = f32[2,8,16,16,16]{3,2,4,1,0:T(8,128)} copy(f32[2,8,16,16,16]{4,3,0,1,2:T(8,128)S(1)} %bitcast.67) | data formatting | bytes 524288 | tf_op jit(solution)/shard_map/all_to_all | solution.py:366
  33.0 2.5 %all_to_all.55 = f32[2,8,256,16]{2,3,1,0:T(8,128)S(1)} reshape(f32[2,8,16,16,16]{3,2,4,1,0:T(8,128)} %copy.21) | data formatting | bytes 524288 | tf_op jit(solution)/shard_map/all_to_all | solution.py:366
  35.9 1.3 %copy.22 = f32[2,8,256,16]{3,1,0,2:T(8,128)S(1)} copy(f32[2,8,256,16]{2,3,1,0:T(8,128)S(1)} %convolution_bitcast_fusion.1) | data formatting | bytes 524288 | tf_op jit(solution)/shard_map/transpose | solution.py:361
  37.2 1.5 %reshape.50 = f32[16,1,4096]{2,1,0:T(1,128)} reshape(f32[256,2,8,16]{3,2,1,0:T(8,128)S(1)} %bitcast.62) | data formatting | bytes 524288
  38.7 11.8 %all-to-all-start.1 = ((f32[16,1,4096]{2,1,0:T(1,128)}), f32[16,1,4096]{2,1,0:T(1,128)S(1)}, u32[]{:S(2)}, u32[]{:S(2)}) async-start(f32[16,1,4096]{2,1,0:T(1,128)} %reshape.50), calls=%async_computation.1 | async-start | bytes 524288 | tf_op jit(solution)/shard_map/all_to_all | solution.py:368
  50.8 10.2 %all-to-all-done.1 = f32[16,1,4096]{2,1,0:T(1,128)S(1)} async-done(((f32[16,1,4096]{2,1,0:T(1,128)}), f32[16,1,4096]{2,1,0:T(1,128)S(1)}, u32[]{:S(2)}, u32[]{:S(2)}) %all-to-all-start.1) | async-done | bytes 262176 | tf_op jit(solution)/shard_map/all_to_all | solution.py:368
  61.0 1.2 %reduce.1 = f32[16,4096]{1,0:T(8,128)S(1)} reduce(f32[16,1,4096]{2,1,0:T(1,128)S(1)} %all-to-all-done.1, f32[]{:T(128)} %broadcast.32), dimensions={1}, to_apply=%all_to_all.56.reduce_sub_computation | reduce | bytes 524292 | tf_op jit(solution)/shard_map/all_to_all | solution.py:368
  62.2 0.7 reshape.51
  63.0 2.6 %copy.38 = f32[2,8,16,16,16]{4,2,3,1,0:T(8,128)} copy(f32[2,8,16,16,16]{4,1,0,3,2:T(8,128)S(1)} %bitcast.68) | data formatting | bytes 524288 | tf_op jit(solution)/shard_map/all_to_all | solution.py:368
  65.5 2.4 %all_to_all.59 = f32[2,8,16,256]{3,2,1,0:T(8,128)S(1)} reshape(f32[2,8,16,16,16]{4,3,2,1,0:T(8,128)} %bitcast.69) | data formatting | bytes 524288 | tf_op jit(solution)/shard_map/all_to_all | solution.py:368
  68.8 1.3 %copy.24 = f32[2,8,16,256]{2,1,0,3:T(8,128)S(1)} copy(f32[2,8,16,256]{3,2,1,0:T(8,128)S(1)} %fusion.1) | data formatting | bytes 524288 | tf_op jit(solution)/shard_map/dot_general | solution.py:360
  70.0 0.7 reshape.52
  70.8 14.4 %all_to_all.73 = f32[16,1,4096]{2,1,0:T(1,128)S(1)} all-to-all(f32[16,1,4096]{2,1,0:T(1,128)S(1)} %reshape.52), channel_id=1, replica_groups=mesh['unit'=2,'row'=16,'col'=16] {'col'}, dimensions={0} | all-to-all | bytes 524288 | tf_op jit(solution)/shard_map/all_to_all | solution.py:376
  85.2 1.2 %reduce.2 = f32[16,4096]{1,0:T(8,128)S(1)} reduce(f32[16,1,4096]{2,1,0:T(1,128)S(1)} %all_to_all.73, f32[]{:T(128)} %broadcast.32), dimensions={1}, to_apply=%all_to_all.60.reduce_sub_computation | reduce | bytes 524292 | tf_op jit(solution)/shard_map/all_to_all | solution.py:376
  86.5 0.7 reshape.53
  87.2 1.0 copy.25
  88.9 3.4 %convolution_bitcast_fusion = f32[2,8,256,16]{2,3,1,0:T(8,128)S(1)} fusion(f32[2,8,256,16]{3,2,1,0:T(8,128)S(1)} %reshape.35, f32[256,256,1,1]{1,0,3,2:T(8,128)S(1)} %copy-done.2), kind=kOutput, calls=%fused_computation.1 | convolution fusion | flops 201326592 | bytes 786432 | tf_op jit(solution)/shard_map/dot_general | solution.py:360
  92.2 1.3 %copy.27 = f32[2,8,256,16]{3,1,0,2:T(8,128)S(1)} copy(f32[2,8,256,16]{2,3,1,0:T(8,128)S(1)} %convolution_bitcast_fusion) | data formatting | bytes 524288 | tf_op jit(solution)/shard_map/transpose | solution.py:361
  93.5 0.7 reshape.54
  94.3 19.4 %all_to_all.74 = f32[16,1,4096]{2,1,0:T(1,128)S(1)} all-to-all(f32[16,1,4096]{2,1,0:T(1,128)S(1)} %reshape.54), channel_id=1, replica_groups=mesh['unit'=2,'row'=16,'col'=16] {'row'}, dimensions={0} | all-to-all | bytes 524288 | tf_op jit(solution)/shard_map/all_to_all | solution.py:378
  113.7 1.2 %reduce.3 = f32[16,4096]{1,0:T(8,128)S(1)} reduce(f32[16,1,4096]{2,1,0:T(1,128)S(1)} %all_to_all.74, f32[]{:T(128)} %broadcast.32), dimensions={1}, to_apply=%all_to_all.64.reduce_sub_computation | reduce | bytes 524292 | tf_op jit(solution)/shard_map/all_to_all | solution.py:378
  114.9 0.7 reshape.55
  115.7 1.0 copy.28
  117.4 3.4 %convolution_bitcast_fusion.2 = f32[2,128,16,16]{1,2,3,0:T(8,128)S(1)} fusion(f32[2,128,16,16]{2,1,3,0:T(8,128)S(1)} %reshape.38, f32[128,128,1,1]{1,0,3,2:T(8,128)S(1)} %copy-done.3), kind=kOutput, calls=%fused_computation.4 | convolution fusion | flops 100663296 | bytes 589824 | tf_op jit(solution)/shard_map/dot_general | solution.py:360
  120.8 0.8 copy.30
  (23 shorter events, 3.3 us)
Async XLA Ops:
  0.0 1.0 copy-start
  33.0 2.5 %copy-start.1 = (f32[256,256,1,1]{1,0,3,2:T(8,128)S(1)}, f32[256,256,1,1]{1,0,3,2:T(8,128)}, u32[]{:S(2)}) copy-start(f32[256,256,1,1]{1,0,3,2:T(8,128)} %constant.29) | copy-start | bytes 786436
  35.9 14.6 %copy-start.5 = (f32[256]{0:T(256)S(1)}, f32[256]{0:T(256)}, u32[]{:S(2)}) copy-start(f32[256]{0:T(256)} %param.12) | copy-start | bytes 3076
  35.9 14.6 %copy-start.6 = (f32[128]{0:T(128)S(1)}, f32[128]{0:T(128)}, u32[]{:S(2)}) copy-start(f32[128]{0:T(128)} %param.11) | copy-start | bytes 1540
  35.9 14.8 %copy-start.4 = (f32[256]{0:T(256)S(1)}, f32[256]{0:T(256)}, u32[]{:S(2)}) copy-start(f32[256]{0:T(256)} %param.13) | copy-start | bytes 3076
  38.7 22.3 %all-to-all-start.1 = ((f32[16,1,4096]{2,1,0:T(1,128)}), f32[16,1,4096]{2,1,0:T(1,128)S(1)}, u32[]{:S(2)}, u32[]{:S(2)}) async-start(f32[16,1,4096]{2,1,0:T(1,128)} %reshape.50), calls=%async_computation.1 | async-start | bytes 524288 | tf_op jit(solution)/shard_map/all_to_all | solution.py:368
  87.2 1.7 %copy-start.2 = (f32[256,256,1,1]{1,0,3,2:T(8,128)S(1)}, f32[256,256,1,1]{1,0,3,2:T(8,128)}, u32[]{:S(2)}) copy-start(f32[256,256,1,1]{1,0,3,2:T(8,128)} %constant.30) | copy-start | bytes 786436
  115.7 1.7 %copy-start.3 = (f32[128,128,1,1]{1,0,3,2:T(8,128)S(1)}, f32[128,128,1,1]{1,0,3,2:T(8,128)}, u32[]{:S(2)}) copy-start(f32[128,128,1,1]{1,0,3,2:T(8,128)} %constant.31) | copy-start | bytes 196612
where the time goes:
time: 122 us
  blocking collectives  57.5 us (47%)
  local copies, waits for them, and re-layouts  27.5 us (23%)
  starting transfers between devices  11.8 us (10%)
  waiting for transfers between devices  10.2 us (8%)
  matrix products  9.11 us (7%)
  other arithmetic  5.08 us (4%)
    all_to_all x1, blocking collectives, by_lines(): lax.all_to_all(values, 'row', split_axis=1, concat_axis=2, tiled=True)  23.7 us
    all_to_all x1, blocking collectives, by_lines(): lax.all_to_all(values, 'row', split_axis=2, concat_axis=1, tiled=True)  19.4 us
    all_to_all x1, blocking collectives, by_lines(): lax.all_to_all(values, 'col', split_axis=3, concat_axis=2, tiled=True)  14.4 us
    all_to_all x1, starting transfers between devices, by_lines(): lax.all_to_all(values, 'col', split_axis=2, concat_axis=3, tiled=True)  11.8 us
    all_to_all x1, waiting for transfers between devices, by_lines(): lax.all_to_all(values, 'col', split_axis=2, concat_axis=3, tiled=True)  10.2 us
    dot_general x5, matrix products, to_modes(): jnp.tensordot(values, table, axes=([dim], [0]), precision=lax.Precision.H...  7.91 us
    unnamed x22, local copies, waits for them, and re-layouts  7.53 us
    transpose x4, local copies, waits for them, and re-layouts, to_modes(): return jnp.moveaxis(moved, -1, dim)  5.19 us
  transfers between devices with their start and end apart: 1, of which 1 were waited for; matrix products, arithmetic and copies ran while one was open for 0% of the time, Pallas kernels for 0%

commit v1 on v0

v1 whole, which is shorter than its diff:
```python
import functools

import jax
import jax.numpy as jnp
import numpy as np
from jax import lax
from jax.experimental import pallas as pl
from jax.experimental.pallas import tpu as pltpu
from jax.sharding import PartitionSpec as P

MESH = pl.DeviceIdType.MESH
LANES = 128
ROWS = 8
NEAR = 8


def mode_table(count):
    rank = np.arange(count)
    angle = np.pi / (4 * count) * ((2 * rank[:, None] + 1) * (2 * rank[None, :] + 1) % (8 * count))
    return np.cos(angle) * (2.0 / count) ** 0.5


def parts_of(table):
    high = table.astype(jnp.bfloat16)
    low = (table - high.astype(np.float64)).astype(jnp.bfloat16)
    return high, low


def split(values):
    high = values.astype(jnp.bfloat16)
    return high, (values - high.astype(jnp.float32)).astype(jnp.bfloat16)


def dot(a, b, dims=((1,), (0,))):
    return lax.dot_general(a, b, (dims, ((), ())), preferred_element_type=jnp.float32)


def thrice(values, axis):
    high, low = split(values)
    return jnp.concatenate([high, high, low], axis=axis)


def swap_blocks(tiles):
    count = len(tiles)
    block = LANES // count
    which = lax.broadcasted_iota(jnp.int32, tiles[0].shape, 1) // block
    tiles = list(tiles)
    bit = 1
    while bit < count:
        upper = which // bit % 2 == 1
        for i in range(count):
            if i & bit == 0:
                a, b = tiles[i], tiles[i + bit]
                tiles[i] = jnp.where(upper, pltpu.roll(b, bit * block, 1), a)
                tiles[i + bit] = jnp.where(upper, b, pltpu.roll(a, LANES - bit * block, 1))
        bit *= 2
    return tiles


def ring(count):
    return sorted(range(count), key=lambda step: -min(step, count - step))


def kernel(
    sizes, x_hbm, sx_ref, sy_hbm, sz_hbm, wx_hbm, wy_hbm, wzl_hbm, back,
    x_ref, sy_ref, sz_ref, wx_ref, wy_ref, wz_ref,
    send1, recv1, send2, recv2, send3, recv3, send4,
    load_sem, send_sem, recv_sem,
):
    fields, count_x, far_rows, cols_n = sizes
    row, col = lax.axis_index("row"), lax.axis_index("col")
    hi, me = row // NEAR, row % NEAR
    pairs = cols_n // 2
    zc, yc = col // 2, col % 2
    share = count_x // NEAR
    tall = 2 * ROWS

    near_peers = []
    for step in ring(NEAR // 2):
        for flip in (1, 0):
            if step or flip:
                near_peers.append(lax.rem(me // 2 + step, NEAR // 2) * 2 + (me + flip) % 2)
    far_peers = []
    for turn in (1, 0):
        for step in ring(pairs):
            for flip in (1, 0):
                if turn or step or flip:
                    far_peers.append(
                        ((hi + turn) % far_rows, lax.rem(zc + step, pairs) * 2 + (yc + flip) % 2)
                    )

    def near_place(peer):
        return {"row": hi * NEAR + peer, "col": col}

    def far_place(peer):
        return {"row": peer[0] * NEAR + me, "col": peer[1]}

    barrier = pltpu.get_barrier_semaphore()
    for peer in far_peers:
        pl.semaphore_signal(barrier, inc=1, device_id=far_place(peer), device_id_type=MESH)
    for peer in near_peers:
        pl.semaphore_signal(barrier, inc=1, device_id=near_place(peer), device_id_type=MESH)

    loads = [
        pltpu.make_async_copy(source, target, load_sem.at[i])
        for i, (source, target) in enumerate(
            [
                (x_hbm, x_ref),
                (wx_hbm, wx_ref),
                (sy_hbm, sy_ref),
                (sz_hbm, sz_ref),
                (wy_hbm, wy_ref),
                (wzl_hbm, wz_ref),
            ]
        )
    ]
    for load in loads:
        load.start()

    def remote(stage, source, target, where):
        return pltpu.make_async_remote_copy(
            src_ref=source,
            dst_ref=target,
            send_sem=send_sem.at[stage],
            recv_sem=recv_sem.at[stage],
            device_id=where,
            device_id_type=MESH,
        )

    loads[0].wait()
    loads[1].wait()
    modes = dot(wx_ref[...], thrice(x_ref[...], 1), ((1,), (1,)))
    for g in range(NEAR):
        for j in range(2 * fields):
            send1[g, j] = modes[g * share : (g + 1) * share, j * LANES : (j + 1) * LANES]

    pl.semaphore_wait(barrier, len(near_peers) + len(far_peers))

    mine1 = pl.ds(me * share, share)
    for peer in near_peers:
        remote(0, send1.at[peer], recv1.at[:, mine1], near_place(peer)).start()
    recv1[:, mine1] = send1[me]

    for load in loads[2:]:
        load.wait()
    count_y, count_z = sy_ref.shape[1], sz_ref.shape[1]

    def wait_stage(stage, source, target, where):
        copy = remote(stage, source, target, where)
        copy.wait_recv()

    def wait_sent(stage, source, target, where):
        remote(stage, source, target, where).wait_send()

    first = near_place(near_peers[0])
    some = far_place(far_peers[0])
    near_rest = pl.ds(0, NEAR - 1)
    far_rest = pl.ds(0, far_rows * cols_n - 1)

    copies1 = (send1.at[near_rest], send4.at[near_rest], first)
    wait_stage(0, *copies1)

    for q in range(far_rows * cols_n):
        f, k = divmod(q, share)
        for h in range(2):
            send2[q, h] = recv1[f * 2 + h, pl.ds(k, NEAR, stride=share), :]

    def slot2(ref):
        return ref.at[col, pl.ds(hi * 2, 2)]

    for peer in far_peers:
        remote(1, send2.at[peer[0] * cols_n + peer[1]], slot2(recv2), far_place(peer)).start()
    recv2[col, pl.ds(hi * 2, 2)] = send2[hi * cols_n + col]

    rank = lax.broadcasted_iota(jnp.int32, (count_y, count_y), 0)
    natural = (
        (rank // (2 * ROWS * NEAR)) * (2 * ROWS * NEAR)
        + rank % NEAR * (2 * ROWS)
        + rank // (ROWS * NEAR) % 2 * ROWS
        + rank // NEAR % ROWS
    )
    chosen = natural == lax.broadcasted_iota(jnp.int32, (count_y, count_y), 1)
    symbol_y = jnp.sum(jnp.where(chosen, sy_ref[...], 0.0), axis=1, keepdims=True)
    factor = lax.rsqrt(sx_ref[me * share + col] + symbol_y + sz_ref[...])

    copies2 = (send2.at[far_rest], recv3.at[far_rest], some)
    wait_stage(1, *copies2)

    halves = cols_n // ROWS
    tiles_t = far_rows * 2
    grid = [[None] * halves for _ in range(tiles_t * ROWS)]
    for t in range(tiles_t):
        for half in range(halves):
            tiles = [recv2[half * ROWS + i, t] for i in range(ROWS)]
            for y, tile in enumerate(swap_blocks(tiles)):
                grid[t * ROWS + y][half] = tile
    block = jnp.concatenate([jnp.concatenate(r, axis=1) for r in grid], axis=0)
    block = dot(wy_ref[...], thrice(block, 0))
    block = dot(thrice(block, 1), wz_ref[...])
    block = block * factor
    block = dot(thrice(block, 1), wz_ref[...])
    block = dot(wy_ref[...], thrice(block, 0))
    for t in range(tiles_t):
        for half in range(halves):
            tiles = [
                block[(t * ROWS + y) * NEAR : (t * ROWS + y + 1) * NEAR, half * LANES : (half + 1) * LANES]
                for y in range(ROWS)
            ]
            for i, tile in enumerate(swap_blocks(tiles)):
                send3[half * ROWS + i, t] = tile

    mine3 = hi * cols_n + col
    for peer in far_peers:
        remote(
            2, send3.at[peer[1], pl.ds(peer[0] * 2, 2)], recv3.at[mine3], far_place(peer)
        ).start()
    recv3[mine3] = send3[col, pl.ds(hi * 2, 2)]
    wait_sent(0, *copies1)
    wait_sent(1, *copies2)
    copies3 = (send2.at[far_rest], recv3.at[far_rest], some)
    wait_stage(2, *copies3)

    for s in range(NEAR):
        for f in range(fields):
            for h in range(2):
                for k in range(share // ROWS):
                    send4[s, f * 2 + h, k * ROWS : (k + 1) * ROWS] = jnp.concatenate(
                        [
                            recv3[f * share + k * ROWS + r, h, s : s + 1, :]
                            for r in range(ROWS)
                        ],
                        axis=0,
                    )
    for peer in near_peers:
        remote(3, send4.at[peer], back.at[:, mine1], near_place(peer)).start()
    back[:, mine1] = send4[me]
    copies4 = (send4.at[near_rest], send1.at[near_rest], first)
    wait_stage(3, *copies4)
    wait_sent(2, *copies3)
    wait_sent(3, *copies4)


def finish(back_ref, wx_ref, out_ref):
    for j in range(back_ref.shape[0]):
        values = thrice(back_ref[j], 0)
        out_ref[j * LANES : (j + 1) * LANES] = dot(values, wx_ref[...], ((0,), (0,)))


def fused(sizes, tracer, symbol_x, symbol_y, symbol_z):
    fields, count_x, far_rows, cols_n = sizes
    share_y, share_z = tracer.shape[2], tracer.shape[3]
    count_y, count_z = symbol_y.shape[0], symbol_z.shape[0]

    order = np.arange(count_y).reshape(far_rows, NEAR, 2, ROWS).transpose(0, 2, 3, 1).reshape(-1)
    high_x, low_x = parts_of(mode_table(count_x))
    high_y, low_y = parts_of(mode_table(count_y)[order][:, order])
    high_z, low_z = parts_of(mode_table(count_z))
    wide_x = np.concatenate([high_x, low_x, high_x], axis=1)
    tall_x = np.concatenate([high_x, low_x, high_x], axis=0)
    wide_y = np.concatenate([high_y, low_y, high_y], axis=1)
    tall_z = np.concatenate([high_z, low_z, high_z], axis=0)

    values = jnp.transpose(tracer, (0, 2, 3, 1)).reshape(fields * share_y * share_z, count_x)
    hbm = pl.BlockSpec(memory_space=pltpu.HBM)
    vmem = pl.BlockSpec(memory_space=pltpu.VMEM)
    smem = pl.BlockSpec(memory_space=pltpu.SMEM)
    operands = (
        values,
        symbol_x,
        symbol_y.reshape(1, -1),
        symbol_z.reshape(1, -1),
        jnp.asarray(wide_x),
        jnp.asarray(wide_y),
        jnp.asarray(tall_z),
    )
    held = [pltpu.VMEM(o.shape, o.dtype) for i, o in enumerate(operands) if i != 1]
    share = count_x // NEAR
    far = far_rows * cols_n

    def floats(*shape):
        return pltpu.VMEM(shape, jnp.float32)

    near_out = (NEAR, 2 * fields, share, LANES)
    back = pl.pallas_call(
        functools.partial(kernel, sizes),
        out_shape=jax.ShapeDtypeStruct((2 * fields, count_x, LANES), jnp.float32),
        in_specs=[hbm, smem] + [hbm] * 5,
        out_specs=vmem,
        scratch_shapes=held
        + [
            floats(*near_out),
            floats(2 * fields, NEAR * share, LANES),
            floats(far, 2, NEAR, LANES),
            floats(cols_n, 2 * far_rows, NEAR, LANES),
            floats(cols_n, 2 * far_rows, NEAR, LANES),
            floats(far, 2, NEAR, LANES),
            floats(*near_out),
        ]
        + [pltpu.SemaphoreType.DMA((len(held),))]
        + [pltpu.SemaphoreType.DMA((4,))] * 2,
        compiler_params=pltpu.CompilerParams(collective_id=0, has_side_effects=True),
    )(*operands)
    out = pl.pallas_call(
        finish,
        out_shape=jax.ShapeDtypeStruct(values.shape, jnp.float32),
        in_specs=[vmem, vmem],
        out_specs=vmem,
        compiler_params=pltpu.CompilerParams(),
    )(back, jnp.asarray(tall_x))
    out = out.reshape(fields, share_y, share_z, count_x)
    return jnp.transpose(out, (0, 3, 1, 2))


def to_modes(values, dim):
    table = jnp.asarray(mode_table(values.shape[dim]), jnp.float32)
    moved = jnp.tensordot(values, table, axes=([dim], [0]), precision=lax.Precision.HIGHEST)
    return jnp.moveaxis(moved, -1, dim)


def by_lines(values, symbol_x, symbol_y, symbol_z):
    values = to_modes(values, 1)
    values = lax.all_to_all(values, "row", split_axis=1, concat_axis=2, tiled=True)
    values = to_modes(values, 2)
    values = lax.all_to_all(values, "col", split_axis=2, concat_axis=3, tiled=True)
    values = to_modes(values, 3)
    share_x, share_y = values.shape[1], values.shape[2]
    part_x = lax.dynamic_slice_in_dim(symbol_x, lax.axis_index("row") * share_x, share_x)
    part_y = lax.dynamic_slice_in_dim(symbol_y, lax.axis_index("col") * share_y, share_y)
    symbol = part_x[:, None, None] + part_y[None, :, None] + symbol_z[None, None, :]
    values = values * lax.rsqrt(symbol)
    values = to_modes(values, 3)
    values = lax.all_to_all(values, "col", split_axis=3, concat_axis=2, tiled=True)
    values = to_modes(values, 2)
    values = lax.all_to_all(values, "row", split_axis=2, concat_axis=1, tiled=True)
    return to_modes(values, 1)


def solution(mesh):
    rows_n, cols_n = mesh.shape["row"], mesh.shape["col"]

    def shards(tracer, symbol_x, symbol_y, symbol_z):
        fields, count_x, share_y, share_z = tracer.shape
        fits = (
            rows_n == 2 * NEAR
            and cols_n == 2 * ROWS
            and fields == rows_n // NEAR
            and count_x == LANES
            and count_x == NEAR * cols_n
            and share_y == 2 * ROWS
            and share_z == LANES // ROWS
        )
        if not fits:
            return by_lines(tracer, symbol_x, symbol_y, symbol_z)
        sizes = fields, count_x, rows_n // NEAR, cols_n
        return fused(sizes, tracer, symbol_x, symbol_y, symbol_z)

    in_specs = (P("unit", None, "row", "col"), P(), P(), P())
    out_specs = P("unit", None, "row", "col")
    return jax.shard_map(shards, mesh=mesh, in_specs=in_specs, out_specs=out_specs, check_vma=False)
```

time: 122 us -> 51.6 us (0.42)
  the two profiles are of different devices: /device:TPU:8 before, /device:TPU:1 now
where the time goes in v1:
time: 51.6 us; the launch traced here: 51.4 us
  Pallas kernels  51.4 us (100%)
    pallas_call x1, Pallas kernels, fused(): pl.pallas_call(functools.partial(kernel, sizes), out_shape=jax.ShapeDtype...  49.4 us
    pallas_call x1, Pallas kernels, fused(): pl.pallas_call(finish, out_shape=jax.ShapeDtypeStruct(values.shape, jnp.f...  1.98 us

profile of v1, /device:TPU:1, one launch (start us, length us, event | category | flops | bytes accessed | tf_op | source)
XLA Modules:
  0.0 51.4 jit_solution(18408015935180143594)
XLA Ops:
  0.0 49.4 %shard_map.82.back_ref = f32[4,128,128]{2,1,0:T(8,128)} custom-call(f32[512,128]{1,0:T(8,128)} %bitcast.8, f32[128]{0:T(128)} %sx_ref.1, f32[1,256]{1,0:T(1,128)} %bitcast.9, f32[1,256]{1,0:T(1,128)} %bitcast.10, bf16[128,384]{1,0:T(8,128)(2,1)} %constant.8.clone.wx_hbm, bf16[256,768]{1,0:T(8,128)(2,1)} %constant.9.clone.wy_hbm, ...), custom_call_target="tpu_custom_call" | custom-call | tf_op jit(solution)/shard_map/pallas_call | solution.py:284
  49.4 2.0 %shard_map.83 = f32[512,128]{1,0:T(8,128)} custom-call(f32[4,128,128]{2,1,0:T(8,128)} %shard_map.82.back_ref, bf16[384,128]{1,0:T(8,128)(2,1)} %constant.11.clone.wx_ref), custom_call_target="tpu_custom_call" | custom-call | tf_op jit(solution)/shard_map/pallas_call | solution.py:303

commit v2 on v1

--- a/solution.py
+++ b/solution.py
@@ -62,31 +62,36 @@
 
 
 def kernel(
-    sizes, x_hbm, sx_ref, sy_hbm, sz_hbm, wx_hbm, wy_hbm, wzl_hbm, back,
-    x_ref, sy_ref, sz_ref, wx_ref, wy_ref, wz_ref,
+    sizes, x_hbm, sx_ref, sy_hbm, sz_hbm, wx_hbm, wy_hbm, wyt_hbm, wz_hbm, back,
+    x_ref, sy_ref, sz_ref, wx_ref, wy_ref, wyt_ref, wz_ref,
     send1, recv1, send2, recv2, send3, recv3, send4,
     load_sem, send_sem, recv_sem,
 ):
     fields, count_x, far_rows, cols_n = sizes
     row, col = lax.axis_index("row"), lax.axis_index("col")
-    hi, me = row // NEAR, row % NEAR
+    hi, me = row >> 3, row & (NEAR - 1)
     pairs = cols_n // 2
-    zc, yc = col // 2, col % 2
+    xc, core = me >> 1, me & 1
+    zc, yc = col >> 1, col & 1
     share = count_x // NEAR
-    tall = 2 * ROWS
 
     near_peers = []
     for step in ring(NEAR // 2):
         for flip in (1, 0):
             if step or flip:
-                near_peers.append(lax.rem(me // 2 + step, NEAR // 2) * 2 + (me + flip) % 2)
+                near_peers.append(
+                    ((xc + step) & (NEAR // 2 - 1)) * 2 + (1 - core if flip else core)
+                )
     far_peers = []
     for turn in (1, 0):
         for step in ring(pairs):
             for flip in (1, 0):
                 if turn or step or flip:
                     far_peers.append(
-                        ((hi + turn) % far_rows, lax.rem(zc + step, pairs) * 2 + (yc + flip) % 2)
+                        (
+                            1 - hi if turn else hi,
+                            ((zc + step) & (pairs - 1)) * 2 + (1 - yc if flip else yc),
+                        )
                     )
 
     def near_place(peer):
@@ -94,12 +99,6 @@
 
     def far_place(peer):
         return {"row": peer[0] * NEAR + me, "col": peer[1]}
-
-    barrier = pltpu.get_barrier_semaphore()
-    for peer in far_peers:
-        pl.semaphore_signal(barrier, inc=1, device_id=far_place(peer), device_id_type=MESH)
-    for peer in near_peers:
-        pl.semaphore_signal(barrier, inc=1, device_id=near_place(peer), device_id_type=MESH)
 
     loads = [
         pltpu.make_async_copy(source, target, load_sem.at[i])
@@ -110,12 +109,19 @@
                 (sy_hbm, sy_ref),
                 (sz_hbm, sz_ref),
                 (wy_hbm, wy_ref),
-                (wzl_hbm, wz_ref),
+                (wyt_hbm, wyt_ref),
+                (wz_hbm, wz_ref),
             ]
         )
     ]
-    for load in loads:
+    for load in loads[:2]:
         load.start()
+
+    barrier = pltpu.get_barrier_semaphore()
+    for peer in far_peers:
+        pl.semaphore_signal(barrier, inc=1, device_id=far_place(peer), device_id_type=MESH)
+    for peer in near_peers:
+        pl.semaphore_signal(barrier, inc=1, device_id=near_place(peer), device_id_type=MESH)
 
     def remote(stage, source, target, where):
         return pltpu.make_async_remote_copy(
@@ -129,6 +135,8 @@
 
     loads[0].wait()
     loads[1].wait()
+    for load in loads[2:]:
+        load.start()
     modes = dot(wx_ref[...], thrice(x_ref[...], 1), ((1,), (1,)))
     for g in range(NEAR):
         for j in range(2 * fields):
@@ -136,41 +144,51 @@
 
     pl.semaphore_wait(barrier, len(near_peers) + len(far_peers))
 
+    away, home = 1 - hi, hi
+    halves = (away, home)
+    columns = pl.ds(col * 2 * NEAR, 2 * NEAR)
     mine1 = pl.ds(me * share, share)
-    for peer in near_peers:
-        remote(0, send1.at[peer], recv1.at[:, mine1], near_place(peer)).start()
+
+    def pair(half):
+        return pl.ds(half * 2, 2)
+
+    for stage, half in enumerate(halves):
+        for peer in near_peers:
+            remote(
+                stage, send1.at[peer, pair(half)], recv1.at[pair(half), mine1], near_place(peer)
+            ).start()
     recv1[:, mine1] = send1[me]
 
     for load in loads[2:]:
         load.wait()
     count_y, count_z = sy_ref.shape[1], sz_ref.shape[1]
-
-    def wait_stage(stage, source, target, where):
-        copy = remote(stage, source, target, where)
-        copy.wait_recv()
-
-    def wait_sent(stage, source, target, where):
-        remote(stage, source, target, where).wait_send()
-
-    first = near_place(near_peers[0])
-    some = far_place(far_peers[0])
     near_rest = pl.ds(0, NEAR - 1)
-    far_rest = pl.ds(0, far_rows * cols_n - 1)
-
-    copies1 = (send1.at[near_rest], send4.at[near_rest], first)
-    wait_stage(0, *copies1)
-
-    for q in range(far_rows * cols_n):
-        f, k = divmod(q, share)
-        for h in range(2):
-            send2[q, h] = recv1[f * 2 + h, pl.ds(k, NEAR, stride=share), :]
-
-    def slot2(ref):
-        return ref.at[col, pl.ds(hi * 2, 2)]
-
-    for peer in far_peers:
-        remote(1, send2.at[peer[0] * cols_n + peer[1]], slot2(recv2), far_place(peer)).start()
-    recv2[col, pl.ds(hi * 2, 2)] = send2[hi * cols_n + col]
+    one_pair = pl.ds(0, 2)
+    near_copy = (
+        send1.at[near_rest, one_pair],
+        send4.at[near_rest, one_pair],
+        near_place(near_peers[0]),
+    )
+
+    def far_copy(half):
+        count = pl.ds(0, cols_n if half is away else cols_n - 1)
+        return send2.at[count], send2.at[count], far_place(far_peers[0])
+
+    away_peers = far_peers[:cols_n]
+    home_peers = far_peers[cols_n:]
+    for stage, (half, peers) in enumerate(zip(halves, (away_peers, home_peers))):
+        remote(stage, *near_copy).wait_recv()
+        for k in range(cols_n):
+            for h in range(2):
+                send2[half * cols_n + k, h] = recv1[half * 2 + h, pl.ds(k, NEAR, stride=share), :]
+        for peer in peers:
+            remote(
+                2 + stage,
+                send2.at[half * cols_n + peer[1]],
+                recv2.at[hi, col],
+                far_place(peer),
+            ).start()
+    recv2[hi, col] = send2[hi * cols_n + col]
 
     rank = lax.broadcasted_iota(jnp.int32, (count_y, count_y), 0)
     natural = (
@@ -183,61 +201,66 @@
     symbol_y = jnp.sum(jnp.where(chosen, sy_ref[...], 0.0), axis=1, keepdims=True)
     factor = lax.rsqrt(sx_ref[me * share + col] + symbol_y + sz_ref[...])
 
-    copies2 = (send2.at[far_rest], recv3.at[far_rest], some)
-    wait_stage(1, *copies2)
-
-    halves = cols_n // ROWS
-    tiles_t = far_rows * 2
-    grid = [[None] * halves for _ in range(tiles_t * ROWS)]
-    for t in range(tiles_t):
-        for half in range(halves):
-            tiles = [recv2[half * ROWS + i, t] for i in range(ROWS)]
-            for y, tile in enumerate(swap_blocks(tiles)):
-                grid[t * ROWS + y][half] = tile
-    block = jnp.concatenate([jnp.concatenate(r, axis=1) for r in grid], axis=0)
-    block = dot(wy_ref[...], thrice(block, 0))
+    groups = cols_n // ROWS
+
+    def gather(half):
+        rows = [[None] * groups for _ in range(2 * ROWS)]
+        for h in range(2):
+            for g in range(groups):
+                tiles = [recv2[half, g * ROWS + i, h] for i in range(ROWS)]
+                for y, tile in enumerate(swap_blocks(tiles)):
+                    rows[h * ROWS + y][g] = tile
+        return jnp.concatenate([jnp.concatenate(r, axis=1) for r in rows], axis=0)
+
+    block = None
+    for stage, half in ((3, home), (2, away)):
+        remote(stage, *far_copy(half)).wait_recv()
+        term = dot(wy_ref[half], thrice(gather(half), 0))
+        block = term if block is None else block + term
     block = dot(thrice(block, 1), wz_ref[...])
     block = block * factor
     block = dot(thrice(block, 1), wz_ref[...])
-    block = dot(wy_ref[...], thrice(block, 0))
-    for t in range(tiles_t):
-        for half in range(halves):
-            tiles = [
-                block[(t * ROWS + y) * NEAR : (t * ROWS + y + 1) * NEAR, half * LANES : (half + 1) * LANES]
-                for y in range(ROWS)
-            ]
-            for i, tile in enumerate(swap_blocks(tiles)):
-                send3[half * ROWS + i, t] = tile
-
-    mine3 = hi * cols_n + col
-    for peer in far_peers:
-        remote(
-            2, send3.at[peer[1], pl.ds(peer[0] * 2, 2)], recv3.at[mine3], far_place(peer)
-        ).start()
-    recv3[mine3] = send3[col, pl.ds(hi * 2, 2)]
-    wait_sent(0, *copies1)
-    wait_sent(1, *copies2)
-    copies3 = (send2.at[far_rest], recv3.at[far_rest], some)
-    wait_stage(2, *copies3)
-
-    for s in range(NEAR):
-        for f in range(fields):
+    lines = thrice(block, 0)
+    for stage, (half, peers) in enumerate(zip(halves, (away_peers, home_peers))):
+        part = dot(wyt_ref[half], lines)
+        for h in range(2):
+            for g in range(groups):
+                tiles = [
+                    part[(h * ROWS + y) * NEAR : (h * ROWS + y + 1) * NEAR, g * LANES : (g + 1) * LANES]
+                    for y in range(ROWS)
+                ]
+                for i, tile in enumerate(swap_blocks(tiles)):
+                    send3[half, g * ROWS + i, h * NEAR : (h + 1) * NEAR] = tile
+        for peer in peers:
+            remote(
+                4 + stage, send3.at[half, peer[1]], recv3.at[hi, columns], far_place(peer)
+            ).start()
+    recv3[hi, columns] = send3[hi, col]
+
+    for stage, half in ((5, home), (4, away)):
+        remote(stage, *far_copy(half)).wait_recv()
+        for s in range(NEAR):
             for h in range(2):
-                for k in range(share // ROWS):
-                    send4[s, f * 2 + h, k * ROWS : (k + 1) * ROWS] = jnp.concatenate(
-                        [
-                            recv3[f * share + k * ROWS + r, h, s : s + 1, :]
-                            for r in range(ROWS)
-                        ],
-                        axis=0,
-                    )
-    for peer in near_peers:
-        remote(3, send4.at[peer], back.at[:, mine1], near_place(peer)).start()
+                for k in range(cols_n // ROWS):
+                    at = k * ROWS * 2 * NEAR + h * NEAR + s
+                    send4[s, half * 2 + h, k * ROWS : (k + 1) * ROWS] = recv3[
+                        half, pl.ds(at, ROWS, stride=2 * NEAR), :
+                    ]
+        for peer in near_peers:
+            remote(
+                2 + stage, send4.at[peer, pair(half)], back.at[pair(half), mine1], near_place(peer)
+            ).start()
     back[:, mine1] = send4[me]
-    copies4 = (send4.at[near_rest], send1.at[near_rest], first)
-    wait_stage(3, *copies4)
-    wait_sent(2, *copies3)
-    wait_sent(3, *copies4)
+    for stage in (0, 1):
+        remote(stage, *near_copy).wait_send()
+    for stage in (2, 4):
+        remote(stage, *far_copy(away)).wait_send()
+    for stage in (3, 5):
+        remote(stage, *far_copy(home)).wait_send()
+    for stage in (7, 6):
+        remote(stage, *near_copy).wait_recv()
+    for stage in (7, 6):
+        remote(stage, *near_copy).wait_send()
 
 
 def finish(back_ref, wx_ref, out_ref):
@@ -257,7 +280,10 @@
     high_z, low_z = parts_of(mode_table(count_z))
     wide_x = np.concatenate([high_x, low_x, high_x], axis=1)
     tall_x = np.concatenate([high_x, low_x, high_x], axis=0)
-    wide_y = np.concatenate([high_y, low_y, high_y], axis=1)
+    depth = count_y // far_rows
+    cuts = [slice(half * depth, (half + 1) * depth) for half in range(far_rows)]
+    in_y = np.stack([np.concatenate([p[:, c] for p in (high_y, low_y, high_y)], axis=1) for c in cuts])
+    out_y = np.stack([np.concatenate([p[c] for p in (high_y, low_y, high_y)], axis=1) for c in cuts])
     tall_z = np.concatenate([high_z, low_z, high_z], axis=0)
 
     values = jnp.transpose(tracer, (0, 2, 3, 1)).reshape(fields * share_y * share_z, count_x)
@@ -270,7 +296,8 @@
         symbol_y.reshape(1, -1),
         symbol_z.reshape(1, -1),
         jnp.asarray(wide_x),
-        jnp.asarray(wide_y),
+        jnp.asarray(in_y),
+        jnp.asarray(out_y),
         jnp.asarray(tall_z),
     )
     held = [pltpu.VMEM(o.shape, o.dtype) for i, o in enumerate(operands) if i != 1]
@@ -283,21 +310,21 @@
     near_out = (NEAR, 2 * fields, share, LANES)
     back = pl.pallas_call(
         functools.partial(kernel, sizes),
-        out_shape=jax.ShapeDtypeStruct((2 * fields, count_x, LANES), jnp.float32),
-        in_specs=[hbm, smem] + [hbm] * 5,
+        out_shape=pltpu.VMEM((2 * fields, count_x, LANES), jnp.float32),
+        in_specs=[hbm, smem] + [hbm] * 6,
         out_specs=vmem,
         scratch_shapes=held
         + [
             floats(*near_out),
             floats(2 * fields, NEAR * share, LANES),
             floats(far, 2, NEAR, LANES),
-            floats(cols_n, 2 * far_rows, NEAR, LANES),
-            floats(cols_n, 2 * far_rows, NEAR, LANES),
-            floats(far, 2, NEAR, LANES),
+            floats(far_rows, cols_n, 2, NEAR, LANES),
+            floats(far_rows, cols_n, 2 * NEAR, LANES),
+            floats(far_rows, cols_n * 2 * NEAR, LANES),
             floats(*near_out),
         ]
         + [pltpu.SemaphoreType.DMA((len(held),))]
-        + [pltpu.SemaphoreType.DMA((4,))] * 2,
+        + [pltpu.SemaphoreType.DMA((8,))] * 2,
         compiler_params=pltpu.CompilerParams(collective_id=0, has_side_effects=True),
     )(*operands)
     out = pl.pallas_call(
@@ -306,7 +333,7 @@
         in_specs=[vmem, vmem],
         out_specs=vmem,
         compiler_params=pltpu.CompilerParams(),
-    )(back, jnp.asarray(tall_x))
+    )(pltpu.with_memory_space_constraint(back, pltpu.VMEM), jnp.asarray(tall_x))
     out = out.reshape(fields, share_y, share_z, count_x)
     return jnp.transpose(out, (0, 3, 1, 2))
 

time: 51.6 us -> 49.2 us (0.953)
  Pallas kernels: 51.4 us -> 49 us
    pallas_call x1, Pallas kernels: 49.4 us -> 47.1 us  [fused(): pl.pallas_call(functools.partial(kernel, sizes), out_shape=pltpu.VMEM((2...]
where the time goes in v2:
time: 49.2 us; the launch traced here: 49 us
  Pallas kernels  49 us (100%)
    pallas_call x1, Pallas kernels, fused(): pl.pallas_call(functools.partial(kernel, sizes), out_shape=pltpu.VMEM((2...  47.1 us
    pallas_call x1, Pallas kernels, fused(): pl.pallas_call(finish, out_shape=jax.ShapeDtypeStruct(values.shape, jnp.f...  1.9 us

profile of v2, /device:TPU:1, one launch (start us, length us, event | category | flops | bytes accessed | tf_op | source)
XLA Modules:
  0.0 49.0 jit_solution(12550233579097783623)
XLA Ops:
  0.0 47.1 %shard_map.91.back_ref = f32[4,128,128]{2,1,0:T(8,128)S(1)} custom-call(f32[512,128]{1,0:T(8,128)} %bitcast.8, f32[128]{0:T(128)} %sx_ref.1, f32[1,256]{1,0:T(1,128)} %bitcast.9, f32[1,256]{1,0:T(1,128)} %bitcast.10, bf16[128,384]{1,0:T(8,128)(2,1)} %constant.10.clone.wx_hbm, bf16[2,256,384]{2,1,0:T(8,128)(2,1)} %constant.11.clone.wy_hbm, ...), custom_call_target="tpu_custom_call" | custom-call | tf_op jit(solution)/shard_map/pallas_call | solution.py:311
  47.1 1.9 %shard_map.92 = f32[512,128]{1,0:T(8,128)} custom-call(f32[4,128,128]{2,1,0:T(8,128)S(1)} %shard_map.91.back_ref, bf16[384,128]{1,0:T(8,128)(2,1)} %constant.14.clone.wx_ref), custom_call_target="tpu_custom_call" | custom-call | tf_op jit(solution)/shard_map/pallas_call | solution.py:330

commit v3 on v2

--- a/solution.py
+++ b/solution.py
@@ -65,7 +65,7 @@
     sizes, x_hbm, sx_ref, sy_hbm, sz_hbm, wx_hbm, wy_hbm, wyt_hbm, wz_hbm, back,
     x_ref, sy_ref, sz_ref, wx_ref, wy_ref, wyt_ref, wz_ref,
     send1, recv1, send2, recv2, send3, recv3, send4,
-    load_sem, send_sem, recv_sem,
+    load_sem, send_sem, recv_sem, near_in, far_in,
 ):
     fields, count_x, far_rows, cols_n = sizes
     row, col = lax.axis_index("row"), lax.axis_index("col")
@@ -117,11 +117,39 @@
     for load in loads[:2]:
         load.start()
 
+    def near_key(peer):
+        return (peer >> 1) * 2 + 1 - (peer & 1)
+
+    def far_key(peer):
+        return ((peer[1] >> 1) * 2 + peer[0] * 5) * 2 + (peer[1] & 1)
+
+    near_mine, far_mine = near_key(me), far_key((hi, col))
+    near_over = [near_key(peer) > near_mine for peer in near_peers]
+    far_over = [far_key(peer) > far_mine for peer in far_peers]
+    near_higher = sum(over.astype(jnp.int32) for over in near_over)
+    far_higher = sum(over.astype(jnp.int32) for over in far_over)
+
     barrier = pltpu.get_barrier_semaphore()
-    for peer in far_peers:
-        pl.semaphore_signal(barrier, inc=1, device_id=far_place(peer), device_id_type=MESH)
-    for peer in near_peers:
-        pl.semaphore_signal(barrier, inc=1, device_id=near_place(peer), device_id_type=MESH)
+
+    def tell(semaphore, where):
+        pl.semaphore_signal(semaphore, inc=1, device_id=where, device_id_type=MESH)
+
+    for peer, over in zip(far_peers, far_over):
+        pl.when(over)(functools.partial(tell, barrier, far_place(peer)))
+    for peer, over in zip(near_peers, near_over):
+        pl.when(over)(functools.partial(tell, barrier, near_place(peer)))
+    lower = len(near_peers) + len(far_peers) - near_higher - far_higher
+
+    @pl.when(lower > 0)
+    def _():
+        pl.semaphore_wait(barrier, lower)
+
+    for peer, over in zip(far_peers, far_over):
+        pl.when(jnp.logical_not(over))(
+            functools.partial(tell, far_in.at[hi * cols_n + col], far_place(peer))
+        )
+    for peer, over in zip(near_peers, near_over):
+        pl.when(jnp.logical_not(over))(functools.partial(tell, near_in, near_place(peer)))
 
     def remote(stage, source, target, where):
         return pltpu.make_async_remote_copy(
@@ -142,7 +170,9 @@
         for j in range(2 * fields):
             send1[g, j] = modes[g * share : (g + 1) * share, j * LANES : (j + 1) * LANES]
 
-    pl.semaphore_wait(barrier, len(near_peers) + len(far_peers))
+    @pl.when(near_higher > 0)
+    def _():
+        pl.semaphore_wait(near_in, near_higher)
 
     away, home = 1 - hi, hi
     halves = (away, home)
@@ -176,18 +206,27 @@
 
     away_peers = far_peers[:cols_n]
     home_peers = far_peers[cols_n:]
-    for stage, (half, peers) in enumerate(zip(halves, (away_peers, home_peers))):
+
+    def outward(peer, stage):
+        remote(
+            stage, send2.at[peer[0] * cols_n + peer[1]], recv2.at[hi, col], far_place(peer)
+        ).start()
+
+    for stage, (half, first) in enumerate(zip(halves, (0, cols_n))):
         remote(stage, *near_copy).wait_recv()
         for k in range(cols_n):
             for h in range(2):
                 send2[half * cols_n + k, h] = recv1[half * 2 + h, pl.ds(k, NEAR, stride=share), :]
-        for peer in peers:
-            remote(
-                2 + stage,
-                send2.at[half * cols_n + peer[1]],
-                recv2.at[hi, col],
-                far_place(peer),
-            ).start()
+        for peer, over in list(zip(far_peers, far_over))[first : first + cols_n]:
+            pl.when(jnp.logical_not(over))(functools.partial(outward, peer, 2 + stage))
+
+    def meet(peer):
+        pl.semaphore_wait(far_in.at[peer[0] * cols_n + peer[1]], 1)
+        outward(peer, 2 + (hi == peer[0]).astype(jnp.int32))
+
+    everyone = [(a, c) for a in range(far_rows) for c in range(cols_n)]
+    for peer in sorted(everyone, key=far_key):
+        pl.when(far_key(peer) > far_mine)(functools.partial(meet, peer))
     recv2[hi, col] = send2[hi * cols_n + col]
 
     rank = lax.broadcasted_iota(jnp.int32, (count_y, count_y), 0)
@@ -324,7 +363,8 @@
             floats(*near_out),
         ]
         + [pltpu.SemaphoreType.DMA((len(held),))]
-        + [pltpu.SemaphoreType.DMA((8,))] * 2,
+        + [pltpu.SemaphoreType.DMA((8,))] * 2
+        + [pltpu.SemaphoreType.REGULAR, pltpu.SemaphoreType.REGULAR((far,))],
         compiler_params=pltpu.CompilerParams(collective_id=0, has_side_effects=True),
     )(*operands)
     out = pl.pallas_call(

time: 49.2 us -> 49.5 us (level)
  no operation moved by 1% of the time
where the time goes in v3:
time: 49.5 us; the launch traced here: 49.4 us
  Pallas kernels  49.4 us (100%)
    pallas_call x1, Pallas kernels, fused(): pl.pallas_call(functools.partial(kernel, sizes), out_shape=pltpu.VMEM((2...  47.5 us
    pallas_call x1, Pallas kernels, fused(): pl.pallas_call(finish, out_shape=jax.ShapeDtypeStruct(values.shape, jnp.f...  1.9 us

profile of v3, /device:TPU:1, one launch (start us, length us, event | category | flops | bytes accessed | tf_op | source)
XLA Modules:
  0.0 49.4 jit_solution(2206897464623973589)
XLA Ops:
  0.0 47.5 %shard_map.91.back_ref = f32[4,128,128]{2,1,0:T(8,128)S(1)} custom-call(f32[512,128]{1,0:T(8,128)} %bitcast.8, f32[128]{0:T(128)} %sx_ref.1, f32[1,256]{1,0:T(1,128)} %bitcast.9, f32[1,256]{1,0:T(1,128)} %bitcast.10, bf16[128,384]{1,0:T(8,128)(2,1)} %constant.10.clone.wx_hbm, bf16[2,256,384]{2,1,0:T(8,128)(2,1)} %constant.11.clone.wy_hbm, ...), custom_call_target="tpu_custom_call" | custom-call | tf_op jit(solution)/shard_map/pallas_call | solution.py:350
  47.5 1.9 %shard_map.92 = f32[512,128]{1,0:T(8,128)} custom-call(f32[4,128,128]{2,1,0:T(8,128)S(1)} %shard_map.91.back_ref, bf16[384,128]{1,0:T(8,128)(2,1)} %constant.14.clone.wx_ref), custom_call_target="tpu_custom_call" | custom-call | tf_op jit(solution)/shard_map/pallas_call | solution.py:370

commit v4 on v2

v4 whole, which is shorter than its diff:
```python
import functools

import jax
import jax.numpy as jnp
import numpy as np
from jax import lax
from jax.experimental import pallas as pl
from jax.experimental.pallas import tpu as pltpu
from jax.sharding import PartitionSpec as P

MESH = pl.DeviceIdType.MESH
LANES = 128
ROWS = 8
NEAR = 8


def mode_table(count):
    rank = np.arange(count)
    angle = np.pi / (4 * count) * ((2 * rank[:, None] + 1) * (2 * rank[None, :] + 1) % (8 * count))
    return np.cos(angle) * (2.0 / count) ** 0.5


def parts_of(table):
    high = table.astype(jnp.bfloat16)
    low = (table - high.astype(np.float64)).astype(jnp.bfloat16)
    return high, low


def split(values):
    high = values.astype(jnp.bfloat16)
    return high, (values - high.astype(jnp.float32)).astype(jnp.bfloat16)


def dot(a, b, dims=((1,), (0,))):
    return lax.dot_general(a, b, (dims, ((), ())), preferred_element_type=jnp.float32)


def thrice(values, axis):
    high, low = split(values)
    return jnp.concatenate([high, high, low], axis=axis)


def swap_blocks(tiles):
    count = len(tiles)
    block = LANES // count
    which = lax.broadcasted_iota(jnp.int32, tiles[0].shape, 1) // block
    tiles = list(tiles)
    bit = 1
    while bit < count:
        upper = which // bit % 2 == 1
        for i in range(count):
            if i & bit == 0:
                a, b = tiles[i], tiles[i + bit]
                tiles[i] = jnp.where(upper, pltpu.roll(b, bit * block, 1), a)
                tiles[i + bit] = jnp.where(upper, b, pltpu.roll(a, LANES - bit * block, 1))
        bit *= 2
    return tiles


def ring(count):
    return sorted(range(count), key=lambda step: -min(step, count - step))


def kernel(
    sizes, x_hbm, sx_ref, sy_hbm, sz_hbm, wx_hbm, wy_hbm, wz_hbm, last_hbm,
    back_p, back_q, last_ref,
    x_ref, sy_ref, sz_ref, wx_ref, wy_ref, wz_ref,
    send_p1, recv_p1, send_q1, recv_q1, send_p2, plane, send_q2, recv_q2,
    result, recv_p3, send_q3, recv_q3, send_q4, send_p4,
    load_sem, send_sem, recv_sem,
):
    fields, count_x, far_rows, cols_n = sizes
    row, col = lax.axis_index("row"), lax.axis_index("col")
    hi, me = row >> 3, row & (NEAR - 1)
    xc, core = me >> 1, me & 1
    zc, yc = col >> 1, col & 1
    pairs, wide = cols_n // 2, NEAR // 2
    far = far_rows * cols_n
    mine = hi * cols_n + col
    in_p = core == yc
    in_q = core != yc

    near_peers = []
    for step in ring(wide):
        for flip in (1, 0):
            if step or flip:
                near_peers.append(((xc + step) & (wide - 1)) * 2 + (1 - core if flip else core))
    far_peers = []
    for turn in (1, 0):
        for step in ring(pairs):
            for flip in (1, 0):
                if turn or step or flip:
                    far_peers.append(
                        (
                            1 - hi if turn else hi,
                            ((zc + step) & (pairs - 1)) * 2 + (1 - yc if flip else yc),
                        )
                    )

    def near_place(peer):
        return {"row": hi * NEAR + peer, "col": col}

    def far_place(peer):
        return {"row": peer[0] * NEAR + me, "col": peer[1]}

    def number(peer):
        return peer[0] * cols_n + peer[1]

    loads = [
        pltpu.make_async_copy(source, target, load_sem.at[i])
        for i, (source, target) in enumerate(
            [
                (x_hbm, x_ref),
                (wx_hbm, wx_ref),
                (sy_hbm, sy_ref),
                (sz_hbm, sz_ref),
                (wy_hbm, wy_ref),
                (wz_hbm, wz_ref),
                (last_hbm, last_ref),
            ]
        )
    ]
    for load in loads[:2]:
        load.start()

    barrier = pltpu.get_barrier_semaphore()
    for peer in far_peers:
        pl.semaphore_signal(barrier, inc=1, device_id=far_place(peer), device_id_type=MESH)
    for peer in near_peers:
        pl.semaphore_signal(barrier, inc=1, device_id=near_place(peer), device_id_type=MESH)

    def remote(stage, source, target, where):
        return pltpu.make_async_remote_copy(
            src_ref=source,
            dst_ref=target,
            send_sem=send_sem.at[stage],
            recv_sem=recv_sem.at[stage],
            device_id=where,
            device_id_type=MESH,
        )

    def total(stage, ref, count):
        some = ref.at[pl.ds(0, count)]
        return remote(stage, some, some, far_place(far_peers[0]))

    def got(stage, ref, count):
        total(stage, ref, count).wait_recv()

    def sent(stage, ref, count):
        total(stage, ref, count).wait_send()

    loads[0].wait()
    loads[1].wait()
    for load in loads[2:]:
        load.start()
    modes = dot(wx_ref[...], thrice(x_ref[...], 1), ((1,), (1,)))
    middle = count_x // 2
    for f in range(fields):
        for c in range(cols_n):
            at = middle + c * wide
            send_q1[f * cols_n + c] = jnp.concatenate(
                [
                    modes[at : at + wide, (f * 2 + h) * LANES : (f * 2 + h + 1) * LANES]
                    for h in range(2)
                ],
                axis=0,
            )
    for n in range(NEAR):
        for j in range(2 * fields):
            send_p1[n, j] = modes[n * ROWS : (n + 1) * ROWS, j * LANES : (j + 1) * LANES]

    pl.semaphore_wait(barrier, len(near_peers) + len(far_peers))

    for peer in far_peers:
        remote(
            0, send_q1.at[number(peer)], recv_q1.at[pl.ds(mine * ROWS, ROWS)], far_place(peer)
        ).start()
    mine_p = pl.ds(me * ROWS, ROWS)
    for peer in near_peers:
        remote(1, send_p1.at[peer], recv_p1.at[:, mine_p], near_place(peer)).start()
    recv_p1[:, mine_p] = send_p1[me]
    recv_q1[pl.ds(mine * ROWS, ROWS)] = send_q1[mine]

    got(1, send_p1, NEAR - 1)
    for f in range(fields):
        for m in range(pairs):
            for h in range(2):
                send_p2[f * pairs + m, h] = recv_p1[f * 2 + h, pl.ds(m, NEAR, stride=ROWS), :]

    def onward_p(peer):
        return remote(
            2,
            send_p2.at[peer[0] * pairs + (peer[1] >> 1)],
            plane.at[hi, col],
            far_place(peer),
        )

    for turn in (1, 0):
        for step in ring(pairs):
            if turn or step:
                place = 1 - hi if turn else hi
                onward_p((place, ((zc + step) & (pairs - 1)) * 2 + core)).start()

    @pl.when(in_q)
    def _():
        onward_p((hi, zc * 2 + core)).start()

    @pl.when(in_p)
    def _():
        plane[hi, col] = send_p2[hi * pairs + zc]

    got(0, send_q1, far - 1)
    for w in range(wide):
        for k in range(far * 2 // ROWS):
            send_q2[w, k * ROWS : (k + 1) * ROWS] = recv_q1[
                pl.ds(k * ROWS * wide + w, ROWS, stride=wide), :
            ]
    span = far * 2
    mine_q = pl.ds(me * span, span)

    def onward_q(x, c):
        return remote(3, send_q2.at[x], recv_q2.at[mine_q], near_place(x * 2 + c))

    for step in ring(wide):
        if step:
            onward_q((xc + step) & (wide - 1), 1 - yc).start()

    @pl.when(in_p)
    def _():
        onward_q(xc, 1 - yc).start()

    @pl.when(in_q)
    def _():
        recv_q2[mine_q] = send_q2[xc]

    for load in loads[2:]:
        load.wait()
    count_y, count_z = sy_ref.shape[1], sz_ref.shape[1]
    rank = lax.broadcasted_iota(jnp.int32, (count_y, count_y), 0)
    natural = (
        (rank // (2 * ROWS * NEAR)) * (2 * ROWS * NEAR)
        + rank % NEAR * (2 * ROWS)
        + rank // (ROWS * NEAR) % 2 * ROWS
        + rank // NEAR % ROWS
    )
    chosen = natural == lax.broadcasted_iota(jnp.int32, (count_y, count_y), 1)
    symbol_y = jnp.sum(jnp.where(chosen, sy_ref[...], 0.0), axis=1, keepdims=True)
    mode = jnp.where(in_p, me * ROWS + zc, middle + col * wide + xc)
    factor = lax.rsqrt(sx_ref[mode] + symbol_y + sz_ref[...])

    @pl.when(in_p)
    def _():
        got(2, result, (far - 1) * 2 * NEAR)

    @pl.when(in_q)
    def _():
        got(3, recv_q2, (NEAR - 1) * span)
        for a in range(far_rows):
            for c in range(cols_n):
                for h in range(2):
                    at = (a * cols_n + c) * 2 + h
                    plane[a, c, h] = recv_q2[pl.ds(at, NEAR, stride=span), :]

    groups = cols_n // ROWS

    def gather(half):
        lines = [[None] * groups for _ in range(2 * ROWS)]
        for h in range(2):
            for g in range(groups):
                tiles = [plane[half, g * ROWS + i, h] for i in range(ROWS)]
                for y, tile in enumerate(swap_blocks(tiles)):
                    lines[h * ROWS + y][g] = tile
        return jnp.concatenate([jnp.concatenate(r, axis=1) for r in lines], axis=0)

    block = dot(wy_ref[...], thrice(jnp.concatenate([gather(0), gather(1)], axis=0), 0))
    block = dot(thrice(block, 1), wz_ref[...])
    block = block * factor
    block = dot(thrice(block, 1), wz_ref[...])
    block = dot(wy_ref[...], thrice(block, 0))
    for a in range(far_rows):
        for h in range(2):
            for g in range(groups):
                first = (a * 2 + h) * ROWS
                tiles = [
                    block[(first + y) * NEAR : (first + y + 1) * NEAR, g * LANES : (g + 1) * LANES]
                    for y in range(ROWS)
                ]
                for i, tile in enumerate(swap_blocks(tiles)):
                    at = (a * cols_n + g * ROWS + i) * 2 * NEAR + h * NEAR
                    result[at : at + NEAR] = tile

    tall = 2 * NEAR

    @pl.when(in_p)
    def _():
        slot = pl.ds((hi * pairs + zc) * tall, tall)
        for peer in far_peers:
            remote(
                4, result.at[pl.ds(number(peer) * tall, tall)], recv_p3.at[slot], far_place(peer)
            ).start()
        recv_p3[slot] = result[pl.ds(mine * tall, tall)]

    @pl.when(in_q)
    def _():
        for s in range(NEAR):
            for h in range(2):
                for k in range(far // ROWS):
                    at = h * far + k * ROWS
                    send_q3[s, at : at + ROWS] = result[
                        pl.ds(k * ROWS * tall + h * NEAR + s, ROWS, stride=tall), :
                    ]
        slot = pl.ds(xc * span, span)
        for peer in near_peers:
            remote(5, send_q3.at[peer], recv_q3.at[slot], near_place(peer)).start()
        recv_q3[slot] = send_q3[me]

    @pl.when(in_p)
    def _():
        got(5, recv_q2, wide * span)

    @pl.when(in_q)
    def _():
        got(5, recv_q2, (wide - 1) * span)

    for q in range(far):
        send_q4[q] = recv_q3[pl.ds(q, ROWS, stride=far), :]
    for peer in far_peers:
        remote(
            6, send_q4.at[number(peer)], back_q.at[pl.ds(mine * ROWS, ROWS)], far_place(peer)
        ).start()
    back_q[pl.ds(mine * ROWS, ROWS)] = send_q4[mine]

    @pl.when(in_p)
    def _():
        got(4, result, (far // 2 - 1) * tall)

    @pl.when(in_q)
    def _():
        got(4, result, far // 2 * tall)

    for s in range(NEAR):
        for f in range(fields):
            for h in range(2):
                send_p4[s, f * 2 + h] = recv_p3[
                    pl.ds(f * pairs * tall + h * NEAR + s, ROWS, stride=tall), :
                ]
    for peer in near_peers:
        remote(7, send_p4.at[peer], back_p.at[:, mine_p], near_place(peer)).start()
    back_p[:, mine_p] = send_p4[me]

    sent(0, send_q1, far - 1)
    sent(1, send_p1, NEAR - 1)

    @pl.when(in_p)
    def _():
        sent(2, result, (far // 2 - 1) * tall)
        sent(3, recv_q2, wide * span)
        sent(4, result, (far - 1) * tall)

    @pl.when(in_q)
    def _():
        sent(2, result, far // 2 * tall)
        sent(3, recv_q2, (wide - 1) * span)
        sent(5, recv_q2, (NEAR - 1) * span)

    got(6, send_q1, far - 1)
    got(7, send_p1, NEAR - 1)
    sent(6, send_q1, far - 1)
    sent(7, send_p1, NEAR - 1)


def finish(cols_n, back_p, back_q, table, out_hbm, held, sems):
    copies = []
    for j in range(back_p.shape[0]):
        f, h = divmod(j, 2)
        tops = [
            back_q[pl.ds((f * cols_n + c) * ROWS + h, ROWS, stride=2), :]
            for c in range(0, cols_n, 2)
        ]
        values = jnp.concatenate([back_p[j]] + tops, axis=0)
        held[j] = dot(thrice(values, 0), table[...], ((0,), (0,)))
        copy = pltpu.make_async_copy(held.at[j], out_hbm.at[pl.ds(j * LANES, LANES)], sems.at[j])
        copy.start()
        copies.append(copy)
    for copy in copies:
        copy.wait()


def fused(sizes, tracer, symbol_x, symbol_y, symbol_z):
    fields, count_x, far_rows, cols_n = sizes
    share_y, share_z = tracer.shape[2], tracer.shape[3]
    count_y, count_z = symbol_y.shape[0], symbol_z.shape[0]

    order = np.arange(count_y).reshape(far_rows, NEAR, 2, ROWS).transpose(0, 2, 3, 1).reshape(-1)
    high_x, low_x = parts_of(mode_table(count_x))
    high_y, low_y = parts_of(mode_table(count_y)[order][:, order])
    high_z, low_z = parts_of(mode_table(count_z))
    wide_x = np.concatenate([high_x, low_x, high_x], axis=1)
    tall_x = np.concatenate([high_x, low_x, high_x], axis=0)
    wide_y = np.concatenate([high_y, low_y, high_y], axis=1)
    tall_z = np.concatenate([high_z, low_z, high_z], axis=0)

    values = jnp.transpose(tracer, (0, 2, 3, 1)).reshape(fields * share_y * share_z, count_x)
    hbm = pl.BlockSpec(memory_space=pltpu.HBM)
    vmem = pl.BlockSpec(memory_space=pltpu.VMEM)
    smem = pl.BlockSpec(memory_space=pltpu.SMEM)
    operands = (
        values,
        symbol_x,
        symbol_y.reshape(1, -1),
        symbol_z.reshape(1, -1),
        jnp.asarray(wide_x),
        jnp.asarray(wide_y),
        jnp.asarray(tall_z),
        jnp.asarray(tall_x),
    )
    held = [pltpu.VMEM(o.shape, o.dtype) for i, o in enumerate(operands[:-1]) if i != 1]
    far = far_rows * cols_n

    def floats(*shape):
        return pltpu.VMEM(shape, jnp.float32)

    near_p = floats(NEAR, 2 * fields, ROWS, LANES)
    far_q = floats(far, ROWS, LANES)
    joined = floats(2 * fields, NEAR * ROWS, LANES)
    pile = floats(far * ROWS, LANES)
    handed = pl.pallas_call(
        functools.partial(kernel, sizes),
        out_shape=(joined, pile, pltpu.VMEM(tall_x.shape, jnp.bfloat16)),
        in_specs=[hbm, smem] + [hbm] * (len(operands) - 2),
        out_specs=(vmem, vmem, vmem),
        scratch_shapes=held
        + [
            near_p,
            joined,
            far_q,
            pile,
            floats(far // 2, 2, NEAR, LANES),
            floats(far_rows, cols_n, 2, NEAR, LANES),
            floats(NEAR // 2, far * 2, LANES),
            floats(NEAR * far * 2, LANES),
            floats(far * 2 * NEAR, LANES),
            floats(far * NEAR, LANES),
            floats(NEAR, far * 2, LANES),
            floats(NEAR // 2 * far * 2, LANES),
            far_q,
            near_p,
        ]
        + [pltpu.SemaphoreType.DMA((len(held) + 1,))]
        + [pltpu.SemaphoreType.DMA((8,))] * 2,
        compiler_params=pltpu.CompilerParams(collective_id=0, has_side_effects=True),
    )(*operands)
    out = pl.pallas_call(
        functools.partial(finish, cols_n),
        out_shape=jax.ShapeDtypeStruct(values.shape, jnp.float32),
        in_specs=[vmem] * 3,
        out_specs=hbm,
        scratch_shapes=[
            floats(2 * fields, LANES, LANES),
            pltpu.SemaphoreType.DMA((2 * fields,)),
        ],
    )(*[pltpu.with_memory_space_constraint(part, pltpu.VMEM) for part in handed])
    out = out.reshape(fields, share_y, share_z, count_x)
    return jnp.transpose(out, (0, 3, 1, 2))


def to_modes(values, dim):
    table = jnp.asarray(mode_table(values.shape[dim]), jnp.float32)
    moved = jnp.tensordot(values, table, axes=([dim], [0]), precision=lax.Precision.HIGHEST)
    return jnp.moveaxis(moved, -1, dim)


def by_lines(values, symbol_x, symbol_y, symbol_z):
    values = to_modes(values, 1)
    values = lax.all_to_all(values, "row", split_axis=1, concat_axis=2, tiled=True)
    values = to_modes(values, 2)
    values = lax.all_to_all(values, "col", split_axis=2, concat_axis=3, tiled=True)
    values = to_modes(values, 3)
    share_x, share_y = values.shape[1], values.shape[2]
    part_x = lax.dynamic_slice_in_dim(symbol_x, lax.axis_index("row") * share_x, share_x)
    part_y = lax.dynamic_slice_in_dim(symbol_y, lax.axis_index("col") * share_y, share_y)
    symbol = part_x[:, None, None] + part_y[None, :, None] + symbol_z[None, None, :]
    values = values * lax.rsqrt(symbol)
    values = to_modes(values, 3)
    values = lax.all_to_all(values, "col", split_axis=3, concat_axis=2, tiled=True)
    values = to_modes(values, 2)
    values = lax.all_to_all(values, "row", split_axis=2, concat_axis=1, tiled=True)
    return to_modes(values, 1)


def solution(mesh):
    rows_n, cols_n = mesh.shape["row"], mesh.shape["col"]

    def shards(tracer, symbol_x, symbol_y, symbol_z):
        fields, count_x, share_y, share_z = tracer.shape
        fits = (
            rows_n == 2 * NEAR
            and cols_n == 2 * ROWS
            and fields == rows_n // NEAR
            and count_x == LANES
            and count_x == NEAR * cols_n
            and share_y == 2 * ROWS
            and share_z == LANES // ROWS
        )
        if not fits:
            return by_lines(tracer, symbol_x, symbol_y, symbol_z)
        sizes = fields, count_x, rows_n // NEAR, cols_n
        return fused(sizes, tracer, symbol_x, symbol_y, symbol_z)

    in_specs = (P("unit", None, "row", "col"), P(), P(), P())
    out_specs = P("unit", None, "row", "col")
    return jax.shard_map(shards, mesh=mesh, in_specs=in_specs, out_specs=out_specs, check_vma=False)
```

time: 49.2 us -> 45.6 us (0.927)
  the two profiles are of different devices: /device:TPU:1 before, /device:TPU:9 now
where the time goes in v4:
time: 45.6 us; the launch traced here: 45.4 us
  Pallas kernels  45.4 us (100%)
    pallas_call x1, Pallas kernels, fused(): pl.pallas_call(functools.partial(kernel, sizes), out_shape=(joined, pile,...  44.4 us
    pallas_call x1, Pallas kernels, fused(): pl.pallas_call(functools.partial(finish, cols_n), out_shape=jax.ShapeDtyp...  0.97 us

profile of v4, /device:TPU:9, one launch (start us, length us, event | category | flops | bytes accessed | tf_op | source)
XLA Modules:
  0.0 45.4 jit_solution(12834693858709996546)
XLA Ops:
  0.0 44.4 %shard_map.82 = (f32[4,64,128]{2,1,0:T(8,128)S(1)}, f32[256,128]{1,0:T(8,128)S(1)}, bf16[384,128]{1,0:T(8,128)(2,1)S(1)}) custom-call(f32[512,128]{1,0:T(8,128)} %bitcast.8, f32[128]{0:T(128)} %sx_ref.1, f32[1,256]{1,0:T(1,128)} %bitcast.9, f32[1,256]{1,0:T(1,128)} %bitcast.10, bf16[128,384]{1,0:T(8,128)(2,1)} %constant.8.clone.wx_hbm, ...), custom_call_target="tpu_custom_call" | custom-call | tf_op jit(solution)/shard_map/pallas_call | solution.py:427
  44.4 1.0 %shard_map.83 = f32[512,128]{1,0:T(8,128)} custom-call(f32[4,64,128]{2,1,0:T(8,128)S(1)} %get-tuple-element.8.back_p, f32[256,128]{1,0:T(8,128)S(1)} %get-tuple-element.9.back_q, bf16[384,128]{1,0:T(8,128)(2,1)S(1)} %get-tuple-element.10.table), custom_call_target="tpu_custom_call" | custom-call | tf_op jit(solution)/shard_map/pallas_call | solution.py:453

commit v5 on v4

--- a/solution.py
+++ b/solution.py
@@ -62,9 +62,9 @@
 
 
 def kernel(
-    sizes, x_hbm, sx_ref, sy_hbm, sz_hbm, wx_hbm, wy_hbm, wz_hbm, last_hbm,
+    sizes, x_hbm, sx_hbm, sy_hbm, sz_hbm, wx_hbm, wy_hbm, wz_hbm, last_hbm,
     back_p, back_q, last_ref,
-    x_ref, sy_ref, sz_ref, wx_ref, wy_ref, wz_ref,
+    x_ref, sx_ref, sy_ref, sz_ref, wx_ref, wy_ref, wz_ref,
     send_p1, recv_p1, send_q1, recv_q1, send_p2, plane, send_q2, recv_q2,
     result, recv_p3, send_q3, recv_q3, send_q4, send_p4,
     load_sem, send_sem, recv_sem,
@@ -112,6 +112,7 @@
             [
                 (x_hbm, x_ref),
                 (wx_hbm, wx_ref),
+                (sx_hbm, sx_ref),
                 (sy_hbm, sy_ref),
                 (sz_hbm, sz_ref),
                 (wy_hbm, wy_ref),
@@ -171,13 +172,19 @@
 
     pl.semaphore_wait(barrier, len(near_peers) + len(far_peers))
 
-    for peer in far_peers:
+    mine_p = pl.ds(me * ROWS, ROWS)
+    for peer in near_peers:
+        remote(1, send_p1.at[peer], recv_p1.at[:, mine_p], near_place(peer)).start()
+    order0 = [(a, c) for a in range(far_rows) for c in range(cols_n)]
+    order0.sort(key=lambda peer: (peer[1] >> 1) * 2 + peer[0] * 5)
+
+    def first0(peer):
         remote(
             0, send_q1.at[number(peer)], recv_q1.at[pl.ds(mine * ROWS, ROWS)], far_place(peer)
         ).start()
-    mine_p = pl.ds(me * ROWS, ROWS)
-    for peer in near_peers:
-        remote(1, send_p1.at[peer], recv_p1.at[:, mine_p], near_place(peer)).start()
+
+    for peer in order0:
+        pl.when(number(peer) != mine)(functools.partial(first0, peer))
     recv_p1[:, mine_p] = send_p1[me]
     recv_q1[pl.ds(mine * ROWS, ROWS)] = send_q1[mine]
 
@@ -246,7 +253,9 @@
     chosen = natural == lax.broadcasted_iota(jnp.int32, (count_y, count_y), 1)
     symbol_y = jnp.sum(jnp.where(chosen, sy_ref[...], 0.0), axis=1, keepdims=True)
     mode = jnp.where(in_p, me * ROWS + zc, middle + col * wide + xc)
-    factor = lax.rsqrt(sx_ref[mode] + symbol_y + sz_ref[...])
+    own = lax.broadcasted_iota(jnp.int32, (1, count_x), 1) == mode
+    symbol_x = jnp.sum(jnp.where(own, sx_ref[...], 0.0), axis=1, keepdims=True)
+    factor = lax.rsqrt(symbol_x + symbol_y + sz_ref[...])
 
     @pl.when(in_p)
     def _():
@@ -290,14 +299,22 @@
                     result[at : at + NEAR] = tile
 
     tall = 2 * NEAR
+    everyone = [(a, c) for a in range(far_rows) for c in range(cols_n)]
+    everyone.sort(key=lambda peer: (peer[1] >> 1) * 2 + peer[0] * 5)
+
+    def each_far(act):
+        for peer in everyone:
+            pl.when(number(peer) != mine)(functools.partial(act, peer))
 
     @pl.when(in_p)
     def _():
         slot = pl.ds((hi * pairs + zc) * tall, tall)
-        for peer in far_peers:
+        def back(peer):
             remote(
                 4, result.at[pl.ds(number(peer) * tall, tall)], recv_p3.at[slot], far_place(peer)
             ).start()
+
+        each_far(back)
         recv_p3[slot] = result[pl.ds(mine * tall, tall)]
 
     @pl.when(in_q)
@@ -324,10 +341,13 @@
 
     for q in range(far):
         send_q4[q] = recv_q3[pl.ds(q, ROWS, stride=far), :]
-    for peer in far_peers:
+
+    def home(peer):
         remote(
             6, send_q4.at[number(peer)], back_q.at[pl.ds(mine * ROWS, ROWS)], far_place(peer)
         ).start()
+
+    each_far(home)
     back_q[pl.ds(mine * ROWS, ROWS)] = send_q4[mine]
 
     @pl.when(in_p)
@@ -403,10 +423,9 @@
     values = jnp.transpose(tracer, (0, 2, 3, 1)).reshape(fields * share_y * share_z, count_x)
     hbm = pl.BlockSpec(memory_space=pltpu.HBM)
     vmem = pl.BlockSpec(memory_space=pltpu.VMEM)
-    smem = pl.BlockSpec(memory_space=pltpu.SMEM)
     operands = (
         values,
-        symbol_x,
+        symbol_x.reshape(1, -1),
         symbol_y.reshape(1, -1),
         symbol_z.reshape(1, -1),
         jnp.asarray(wide_x),
@@ -414,7 +433,7 @@
         jnp.asarray(tall_z),
         jnp.asarray(tall_x),
     )
-    held = [pltpu.VMEM(o.shape, o.dtype) for i, o in enumerate(operands[:-1]) if i != 1]
+    held = [pltpu.VMEM(o.shape, o.dtype) for o in operands[:-1]]
     far = far_rows * cols_n
 
     def floats(*shape):
@@ -427,7 +446,7 @@
     handed = pl.pallas_call(
         functools.partial(kernel, sizes),
         out_shape=(joined, pile, pltpu.VMEM(tall_x.shape, jnp.bfloat16)),
-        in_specs=[hbm, smem] + [hbm] * (len(operands) - 2),
+        in_specs=[hbm] * len(operands),
         out_specs=(vmem, vmem, vmem),
         scratch_shapes=held
         + [

time: 45.6 us -> 42.9 us (0.941)
  the two profiles are of different devices: /device:TPU:9 before, /device:TPU:1 now
where the time goes in v5:
time: 42.9 us; the launch traced here: 42.8 us
  Pallas kernels  42.8 us (100%)
    pallas_call x1, Pallas kernels, fused(): pl.pallas_call(functools.partial(kernel, sizes), out_shape=(joined, pile,...  41.8 us
    pallas_call x1, Pallas kernels, fused(): pl.pallas_call(functools.partial(finish, cols_n), out_shape=jax.ShapeDtyp...  0.97 us

profile of v5, /device:TPU:1, one launch (start us, length us, event | category | flops | bytes accessed | tf_op | source)
XLA Modules:
  0.0 42.8 jit_solution(5920211241460786225)
XLA Ops:
  0.0 41.8 %shard_map.82 = (f32[4,64,128]{2,1,0:T(8,128)S(1)}, f32[256,128]{1,0:T(8,128)S(1)}, bf16[384,128]{1,0:T(8,128)(2,1)S(1)}) custom-call(f32[512,128]{1,0:T(8,128)} %bitcast.9, f32[1,128]{1,0:T(1,128)} %bitcast.12, f32[1,256]{1,0:T(1,128)} %bitcast.10, f32[1,256]{1,0:T(1,128)} %bitcast.11, bf16[128,384]{1,0:T(8,128)(2,1)} %constant.8.clone.wx_hbm, ...), custom_call_target="tpu_custom_call" | custom-call | tf_op jit(solution)/shard_map/pallas_call | solution.py:446
  41.8 1.0 %shard_map.83 = f32[512,128]{1,0:T(8,128)} custom-call(f32[4,64,128]{2,1,0:T(8,128)S(1)} %get-tuple-element.8.back_p, f32[256,128]{1,0:T(8,128)S(1)} %get-tuple-element.9.back_q, bf16[384,128]{1,0:T(8,128)(2,1)S(1)} %get-tuple-element.10.table), custom_call_target="tpu_custom_call" | custom-call | tf_op jit(solution)/shard_map/pallas_call | solution.py:472

commit v6 on v5

--- a/solution.py
+++ b/solution.py
@@ -77,8 +77,10 @@
     pairs, wide = cols_n // 2, NEAR // 2
     far = far_rows * cols_n
     mine = hi * cols_n + col
-    in_p = core == yc
-    in_q = core != yc
+    even = zc & 1
+    lane = (zc >> 1) * 2 + yc
+    in_p = core == even
+    in_q = core != even
 
     near_peers = []
     for step in ring(wide):
@@ -197,24 +199,27 @@
     def onward_p(peer):
         return remote(
             2,
-            send_p2.at[peer[0] * pairs + (peer[1] >> 1)],
+            send_p2.at[peer[0] * pairs + (peer[1] >> 2) * 2 + (peer[1] & 1)],
             plane.at[hi, col],
             far_place(peer),
         )
 
+    half = pairs // 2
     for turn in (1, 0):
-        for step in ring(pairs):
-            if turn or step:
-                place = 1 - hi if turn else hi
-                onward_p((place, ((zc + step) & (pairs - 1)) * 2 + core)).start()
-
-    @pl.when(in_q)
-    def _():
-        onward_p((hi, zc * 2 + core)).start()
-
-    @pl.when(in_p)
-    def _():
-        plane[hi, col] = send_p2[hi * pairs + zc]
+        place = 1 - hi if turn else hi
+        for step in ring(half):
+            for flip in (1, 0):
+                if turn or step or flip:
+                    z = (((zc >> 1) + step) & (half - 1)) * 2 + core
+                    onward_p((place, z * 2 + (1 - yc if flip else yc))).start()
+
+    @pl.when(in_q)
+    def _():
+        onward_p((hi, ((zc >> 1) * 2 + core) * 2 + yc)).start()
+
+    @pl.when(in_p)
+    def _():
+        plane[hi, col] = send_p2[hi * pairs + lane]
 
     got(0, send_q1, far - 1)
     for w in range(wide):
@@ -230,11 +235,11 @@
 
     for step in ring(wide):
         if step:
-            onward_q((xc + step) & (wide - 1), 1 - yc).start()
-
-    @pl.when(in_p)
-    def _():
-        onward_q(xc, 1 - yc).start()
+            onward_q((xc + step) & (wide - 1), 1 - even).start()
+
+    @pl.when(in_p)
+    def _():
+        onward_q(xc, 1 - even).start()
 
     @pl.when(in_q)
     def _():
@@ -252,7 +257,7 @@
     )
     chosen = natural == lax.broadcasted_iota(jnp.int32, (count_y, count_y), 1)
     symbol_y = jnp.sum(jnp.where(chosen, sy_ref[...], 0.0), axis=1, keepdims=True)
-    mode = jnp.where(in_p, me * ROWS + zc, middle + col * wide + xc)
+    mode = jnp.where(in_p, me * ROWS + lane, middle + col * wide + xc)
     own = lax.broadcasted_iota(jnp.int32, (1, count_x), 1) == mode
     symbol_x = jnp.sum(jnp.where(own, sx_ref[...], 0.0), axis=1, keepdims=True)
     factor = lax.rsqrt(symbol_x + symbol_y + sz_ref[...])
@@ -308,7 +313,7 @@
 
     @pl.when(in_p)
     def _():
-        slot = pl.ds((hi * pairs + zc) * tall, tall)
+        slot = pl.ds((hi * pairs + lane) * tall, tall)
         def back(peer):
             remote(
                 4, result.at[pl.ds(number(peer) * tall, tall)], recv_p3.at[slot], far_place(peer)

time: 42.9 us -> 42.4 us (0.988)
  Pallas kernels: 42.8 us -> 42.3 us
    pallas_call x1, Pallas kernels: 41.8 us -> 41.3 us  [fused(): pl.pallas_call(functools.partial(kernel, sizes), out_shape=(joined, pile,...]
where the time goes in v6:
time: 42.4 us; the launch traced here: 42.3 us
  Pallas kernels  42.3 us (100%)
    pallas_call x1, Pallas kernels, fused(): pl.pallas_call(functools.partial(kernel, sizes), out_shape=(joined, pile,...  41.3 us
    pallas_call x1, Pallas kernels, fused(): pl.pallas_call(functools.partial(finish, cols_n), out_shape=jax.ShapeDtyp...  0.97 us

profile of v6, /device:TPU:1, one launch (start us, length us, event | category | flops | bytes accessed | tf_op | source)
XLA Modules:
  0.0 42.3 jit_solution(9407966667797541534)
XLA Ops:
  0.0 41.3 %shard_map.82 = (f32[4,64,128]{2,1,0:T(8,128)S(1)}, f32[256,128]{1,0:T(8,128)S(1)}, bf16[384,128]{1,0:T(8,128)(2,1)S(1)}) custom-call(f32[512,128]{1,0:T(8,128)} %bitcast.9, f32[1,128]{1,0:T(1,128)} %bitcast.12, f32[1,256]{1,0:T(1,128)} %bitcast.10, f32[1,256]{1,0:T(1,128)} %bitcast.11, bf16[128,384]{1,0:T(8,128)(2,1)} %constant.8.clone.wx_hbm, ...), custom_call_target="tpu_custom_call" | custom-call | tf_op jit(solution)/shard_map/pallas_call | solution.py:451
  41.3 1.0 %shard_map.83 = f32[512,128]{1,0:T(8,128)} custom-call(f32[4,64,128]{2,1,0:T(8,128)S(1)} %get-tuple-element.8.back_p, f32[256,128]{1,0:T(8,128)S(1)} %get-tuple-element.9.back_q, bf16[384,128]{1,0:T(8,128)(2,1)S(1)} %get-tuple-element.10.table), custom_call_target="tpu_custom_call" | custom-call | tf_op jit(solution)/shard_map/pallas_call | solution.py:477

commit v7 on v6

--- a/solution.py
+++ b/solution.py
@@ -178,7 +178,7 @@
     for peer in near_peers:
         remote(1, send_p1.at[peer], recv_p1.at[:, mine_p], near_place(peer)).start()
     order0 = [(a, c) for a in range(far_rows) for c in range(cols_n)]
-    order0.sort(key=lambda peer: (peer[1] >> 1) * 2 + peer[0] * 5)
+    order0.sort(key=lambda peer: (peer[1] >> 1) * 2 + peer[0] * 7)
 
     def first0(peer):
         remote(
@@ -305,7 +305,7 @@
 
     tall = 2 * NEAR
     everyone = [(a, c) for a in range(far_rows) for c in range(cols_n)]
-    everyone.sort(key=lambda peer: (peer[1] >> 1) * 2 + peer[0] * 5)
+    everyone.sort(key=lambda peer: (peer[1] >> 1) * 2 + peer[0] * 3)
 
     def each_far(act):
         for peer in everyone:

time: 42.4 us -> 42.2 us (level)
  no operation moved by 1% of the time
where the time goes in v7:
time: 42.2 us; the launch traced here: 42.1 us
  Pallas kernels  42.1 us (100%)
    pallas_call x1, Pallas kernels, fused(): pl.pallas_call(functools.partial(kernel, sizes), out_shape=(joined, pile,...  41.1 us
    pallas_call x1, Pallas kernels, fused(): pl.pallas_call(functools.partial(finish, cols_n), out_shape=jax.ShapeDtyp...  0.97 us

profile of v7, /device:TPU:1, one launch (start us, length us, event | category | flops | bytes accessed | tf_op | source)
XLA Modules:
  0.0 42.1 jit_solution(6592730608966653290)
XLA Ops:
  0.0 41.1 %shard_map.82 = (f32[4,64,128]{2,1,0:T(8,128)S(1)}, f32[256,128]{1,0:T(8,128)S(1)}, bf16[384,128]{1,0:T(8,128)(2,1)S(1)}) custom-call(f32[512,128]{1,0:T(8,128)} %bitcast.9, f32[1,128]{1,0:T(1,128)} %bitcast.12, f32[1,256]{1,0:T(1,128)} %bitcast.10, f32[1,256]{1,0:T(1,128)} %bitcast.11, bf16[128,384]{1,0:T(8,128)(2,1)} %constant.8.clone.wx_hbm, ...), custom_call_target="tpu_custom_call" | custom-call | tf_op jit(solution)/shard_map/pallas_call | solution.py:451
  41.1 1.0 %shard_map.83 = f32[512,128]{1,0:T(8,128)} custom-call(f32[4,64,128]{2,1,0:T(8,128)S(1)} %get-tuple-element.8.back_p, f32[256,128]{1,0:T(8,128)S(1)} %get-tuple-element.9.back_q, bf16[384,128]{1,0:T(8,128)(2,1)S(1)} %get-tuple-element.10.table), custom_call_target="tpu_custom_call" | custom-call | tf_op jit(solution)/shard_map/pallas_call | solution.py:477

commit v8 on v7

--- a/solution.py
+++ b/solution.py
@@ -311,17 +311,6 @@
         for peer in everyone:
             pl.when(number(peer) != mine)(functools.partial(act, peer))
 
-    @pl.when(in_p)
-    def _():
-        slot = pl.ds((hi * pairs + lane) * tall, tall)
-        def back(peer):
-            remote(
-                4, result.at[pl.ds(number(peer) * tall, tall)], recv_p3.at[slot], far_place(peer)
-            ).start()
-
-        each_far(back)
-        recv_p3[slot] = result[pl.ds(mine * tall, tall)]
-
     @pl.when(in_q)
     def _():
         for s in range(NEAR):
@@ -335,6 +324,17 @@
         for peer in near_peers:
             remote(5, send_q3.at[peer], recv_q3.at[slot], near_place(peer)).start()
         recv_q3[slot] = send_q3[me]
+
+    @pl.when(in_p)
+    def _():
+        slot = pl.ds((hi * pairs + lane) * tall, tall)
+        def back(peer):
+            remote(
+                4, result.at[pl.ds(number(peer) * tall, tall)], recv_p3.at[slot], far_place(peer)
+            ).start()
+
+        each_far(back)
+        recv_p3[slot] = result[pl.ds(mine * tall, tall)]
 
     @pl.when(in_p)
     def _():

time: 42.2 us -> 42.2 us (level)
  no operation moved by 1% of the time
where the time goes in v8:
time: 42.2 us; the launch traced here: 42.1 us
  Pallas kernels  42.1 us (100%)
    pallas_call x1, Pallas kernels, fused(): pl.pallas_call(functools.partial(kernel, sizes), out_shape=(joined, pile,...  41.1 us
    pallas_call x1, Pallas kernels, fused(): pl.pallas_call(functools.partial(finish, cols_n), out_shape=jax.ShapeDtyp...  0.97 us

profile of v8, /device:TPU:1, one launch (start us, length us, event | category | flops | bytes accessed | tf_op | source)
XLA Modules:
  0.0 42.1 jit_solution(421853260264231728)
XLA Ops:
  0.0 41.1 %shard_map.82 = (f32[4,64,128]{2,1,0:T(8,128)S(1)}, f32[256,128]{1,0:T(8,128)S(1)}, bf16[384,128]{1,0:T(8,128)(2,1)S(1)}) custom-call(f32[512,128]{1,0:T(8,128)} %bitcast.9, f32[1,128]{1,0:T(1,128)} %bitcast.12, f32[1,256]{1,0:T(1,128)} %bitcast.10, f32[1,256]{1,0:T(1,128)} %bitcast.11, bf16[128,384]{1,0:T(8,128)(2,1)} %constant.8.clone.wx_hbm, ...), custom_call_target="tpu_custom_call" | custom-call | tf_op jit(solution)/shard_map/pallas_call | solution.py:451
  41.1 1.0 %shard_map.83 = f32[512,128]{1,0:T(8,128)} custom-call(f32[4,64,128]{2,1,0:T(8,128)S(1)} %get-tuple-element.8.back_p, f32[256,128]{1,0:T(8,128)S(1)} %get-tuple-element.9.back_q, bf16[384,128]{1,0:T(8,128)(2,1)S(1)} %get-tuple-element.10.table), custom_call_target="tpu_custom_call" | custom-call | tf_op jit(solution)/shard_map/pallas_call | solution.py:477

commit v9 on v8

--- a/solution.py
+++ b/solution.py
@@ -178,7 +178,7 @@
     for peer in near_peers:
         remote(1, send_p1.at[peer], recv_p1.at[:, mine_p], near_place(peer)).start()
     order0 = [(a, c) for a in range(far_rows) for c in range(cols_n)]
-    order0.sort(key=lambda peer: (peer[1] >> 1) * 2 + peer[0] * 7)
+    order0.sort(key=lambda peer: (peer[1] >> 1) * 2 + peer[0] * 9)
 
     def first0(peer):
         remote(

time: 42.2 us -> 42.3 us (level)
  no operation moved by 1% of the time
where the time goes in v9:
time: 42.3 us; the launch traced here: 42.2 us
  Pallas kernels  42.2 us (100%)
    pallas_call x1, Pallas kernels, fused(): pl.pallas_call(functools.partial(kernel, sizes), out_shape=(joined, pile,...  41.2 us
    pallas_call x1, Pallas kernels, fused(): pl.pallas_call(functools.partial(finish, cols_n), out_shape=jax.ShapeDtyp...  0.97 us

profile of v9, /device:TPU:1, one launch (start us, length us, event | category | flops | bytes accessed | tf_op | source)
XLA Modules:
  0.0 42.2 jit_solution(2689386555363748841)
XLA Ops:
  0.0 41.2 %shard_map.82 = (f32[4,64,128]{2,1,0:T(8,128)S(1)}, f32[256,128]{1,0:T(8,128)S(1)}, bf16[384,128]{1,0:T(8,128)(2,1)S(1)}) custom-call(f32[512,128]{1,0:T(8,128)} %bitcast.9, f32[1,128]{1,0:T(1,128)} %bitcast.12, f32[1,256]{1,0:T(1,128)} %bitcast.10, f32[1,256]{1,0:T(1,128)} %bitcast.11, bf16[128,384]{1,0:T(8,128)(2,1)} %constant.8.clone.wx_hbm, ...), custom_call_target="tpu_custom_call" | custom-call | tf_op jit(solution)/shard_map/pallas_call | solution.py:451
  41.2 1.0 %shard_map.83 = f32[512,128]{1,0:T(8,128)} custom-call(f32[4,64,128]{2,1,0:T(8,128)S(1)} %get-tuple-element.8.back_p, f32[256,128]{1,0:T(8,128)S(1)} %get-tuple-element.9.back_q, bf16[384,128]{1,0:T(8,128)(2,1)S(1)} %get-tuple-element.10.table), custom_call_target="tpu_custom_call" | custom-call | tf_op jit(solution)/shard_map/pallas_call | solution.py:477
